TPU v7x, 32 devices: a whole 2x2x4 slice. The times are simulated.
32 devices in a mesh: dp: 8 (over z, x), tensor: 4 (over y, core).
Axes of the slice: x: 2, y: 2, z: 4, core: 2. Of those that a mesh axis runs over, the one named last changes fastest.
Arguments:
- attn_out: bfloat16 [4096, 2560], P('dp', 'tensor'), may hold values from -6 to 6
- resid: bfloat16 [4096, 5120], P('dp', 'tensor'), may hold values from -6 to 6
- out_proj: bfloat16 [2560, 5120], P('tensor'), may hold values from -0.125 to 0.125
- heads: bfloat16 [5120, 8], P('tensor'), may hold values from -0.078125 to 0.078125
- gain: bfloat16 [5120], P('tensor'), may hold values from 0.25 to 1.75
- lengths: int32 [64], P('dp'), may hold values from 0 to 63
Outputs:
- uwo: float32 [64], P('dp')
- proj_grad: float32 [5120, 2560], P('dp', 'tensor')
- head_grad: float32 [5120, 8], P('tensor')
- gain_grad: float32 [5120], P('tensor')
Inputs may be any that keep to these rules, and one draw needn't show every extreme that they name: Positions 0 to lengths[n] of response n are scored.
All inputs are finite; a program needn't handle non-finite values.
Results may differ from a plain program's by a relative error of at most 0.0085.
Values may be sent and summed in bfloat16 or wider, within the bound.
A program may use at most 128 MiB of HBM per device.

v0:
```python
import jax
import jax.numpy as jnp
from jax import lax
from jax.sharding import PartitionSpec as P

D = 5120


EPS_NORM = 1e-06
EPS_VAR = 1e-05
PENALTY = 0.5


def per_device(attn_out, resid, out_proj, heads, gain, lengths):
    total_rows = attn_out.shape[0]
    resp_dev = lengths.shape[0]
    seq_len = total_rows // resp_dev
    members = heads.shape[1]
    highest = lax.Precision.HIGHEST
    product = jnp.dot(attn_out, out_proj, preferred_element_type=jnp.float32)
    gain_local = gain.astype(jnp.float32)
    heads_local = heads.astype(jnp.float32)
    hidden = resid.astype(jnp.float32) + lax.psum_scatter(
        product.astype(jnp.bfloat16), "tensor", scatter_dimension=1, tiled=True
    ).astype(jnp.float32)
    squares = lax.psum(jnp.sum(hidden * hidden, axis=1), "tensor")
    rinv = lax.rsqrt(squares / D + EPS_NORM)
    normed = hidden * rinv[:, None] * gain_local[None, :]
    scores = lax.psum(jnp.dot(normed, heads_local, precision=highest), "tensor")
    position = lax.broadcasted_iota(jnp.int32, (resp_dev, seq_len), 1)
    inside = position <= lengths[:, None]
    counts = (lengths + 1).astype(jnp.float32)
    per_resp = scores.reshape(resp_dev, seq_len, members)
    rewards = jnp.sum(jnp.where(inside[:, :, None], per_resp, 0.0), axis=1) / counts[:, None]
    total_resp = resp_dev * lax.axis_size("dp")
    first_sum, second_sum = lax.psum(
        (jnp.sum(rewards, axis=0), jnp.sum(rewards * rewards, axis=0)), "dp"
    )
    center = first_sum / total_resp
    spread = second_sum / total_resp - center * center
    zed = (rewards - center[None, :]) * lax.rsqrt(spread + EPS_VAR)[None, :]
    zmean = jnp.mean(zed, axis=1)
    uwo = zmean - PENALTY * jnp.mean((zed - zmean[:, None]) ** 2, axis=1)
    pairs = rewards.reshape(resp_dev // 2, 2, members)
    weight = jax.nn.sigmoid(pairs[:, 1] - pairs[:, 0])
    dreward = jnp.stack([-weight, weight], axis=1).reshape(resp_dev, members)
    dscore = jnp.where(inside[:, :, None], (dreward / counts[:, None])[:, None, :], 0.0).reshape(
        total_rows, members
    )
    dnormed_local = jnp.dot(dscore, heads_local.T, precision=highest)
    inner = lax.psum(jnp.sum(hidden * gain_local[None, :] * dnormed_local, axis=1), "tensor")
    dhidden = (
        rinv[:, None] * gain_local[None, :] * dnormed_local
        - hidden * (rinv**3 * inner / D)[:, None]
    ).astype(jnp.bfloat16)
    head_term = jnp.dot(normed.T, dscore, precision=highest)
    gain_term = jnp.sum(dnormed_local * hidden * rinv[:, None], axis=0)
    head_grad, gain_grad = lax.psum((head_term, gain_term), "dp")
    term = jnp.einsum(
        "rd,rj->dj",
        lax.all_gather(dhidden, "tensor", axis=1, tiled=True),
        attn_out,
        preferred_element_type=jnp.float32,
    )
    proj_grad = lax.psum_scatter(term, "dp", scatter_dimension=0, tiled=True)
    return (uwo, proj_grad, head_grad, gain_grad)


def solution(mesh):
    return jax.shard_map(
        per_device,
        mesh=mesh,
        in_specs=(
            P("dp", "tensor"),
            P("dp", "tensor"),
            P("tensor", None),
            P("tensor", None),
            P("tensor"),
            P("dp"),
        ),
        out_specs=(P("dp"), P("dp", "tensor"), P("tensor", None), P("tensor")),
        check_vma=False,
    )
```

profile of v0, /device:TPU:0, one launch (start us, length us, event | category | flops | bytes accessed | tf_op | source)
XLA Modules:
  0.0 384.5 jit_solution(8206958620141189595)
XLA Ops:
  7.2 0.0 copy-start
  7.2 0.0 reduce-scatter.3.cloned.1.call-start
  7.2 1.0 copy-done
  8.3 8.8 %convolution_convert_fusion = bf16[512,5120]{1,0:T(8,128)(2,1)} fusion(bf16[512,640]{1,0:T(8,128)(2,1)S(1)} %copy-done, bf16[640,5120]{1,0:T(8,128)(2,1)} %param.8), kind=kOutput, calls=%fused_computation | convolution fusion | flops 3358064640 | bytes 12451840 | tf_op jit(solution)/shard_map/dot_general | solution.py:20
  17.1 0.0 reduce-scatter.3.cloned.1.call-update
  17.1 0.0 copy-start.7
  17.1 0.0 all-gather.2.cloned.1.call-start
  17.2 0.6 copy-done.8
  17.7 0.1 iota_compare_fusion
  17.8 0.6 le.18
  18.4 0.1 div.52
  18.5 0.1 copy.14
  18.6 0.0 copy-done.6
  18.6 52.6 %reduce-scatter.3.cloned.1.call-done = bf16[512,1280]{1,0:T(8,128)(2,1)} async-done(((bf16[512,5120]{1,0:T(8,128)(2,1)}), bf16[512,1280]{1,0:T(8,128)(2,1)}) %reduce-scatter.3.cloned.1.call-update) | async-done | bytes 1310736 | tf_op jit(solution)/shard_map/reduce_scatter | solution.py:23
  71.2 0.0 copy-done.1
  71.2 1.9 multiply_reduce_fusion.2
  73.1 5.8 %psum.49 = f32[512]{0:T(512)S(1)} all-reduce(f32[512]{0:T(512)S(1)} %multiply_reduce_fusion.2), channel_id=1, replica_groups=mesh['dp'=8,'tensor'=4] {'tensor'}, use_global_device_ids=true, to_apply=%region_2.0 | all-reduce | flops 512 | bytes 4096 | tf_op jit(solution)/shard_map/psum | solution.py:26
  78.9 0.0 copy-done.7
  78.9 0.0 copy-done.2
  78.9 0.0 copy-start.3
  78.9 1.7 fusion.1
  80.6 0.1 reshape.69
  80.7 0.0 copy-done.3
  80.7 10.3 %psum.50 = f32[8,64,8]{1,0,2:T(8,128)S(1)} all-reduce(f32[8,64,8]{1,0,2:T(8,128)S(1)} %reshape.69), channel_id=1, replica_groups=mesh['dp'=8,'tensor'=4] {'tensor'}, use_global_device_ids=true, to_apply=%region_3.0 | all-reduce | flops 4096 | bytes 32768 | tf_op jit(solution)/shard_map/psum | solution.py:29
  91.0 0.1 select_reduce_fusion
  91.0 0.1 copy.13
  91.1 0.1 copy_divide_fusion
  91.2 0.1 copy.17
  91.3 0.0 copy-done.5
  91.3 0.7 fusion.13
  92.0 0.7 copy.18
  92.7 0.8 bitcast_select_fusion
  93.5 4.6 %multiply_reduce_fusion = (f32[1280]{0:T(1024)}, f32[512]{0:T(512)}, f32[512,1280]{1,0:T(8,128)}) fusion(bf16[512,1280]{1,0:T(8,128)(2,1)S(1)} %copy-done.2, bf16[512,1280]{1,0:T(8,128)(2,1)S(1)} %copy-done.1, f32[512]{0:T(512)} %copy-done.3, f32[1280]{0:T(1024)S(1)} %convert_element_type.22, f32[512,8]{1,0:T(8,128)S(1)} %bitcast_select_fusion, ...), kind=kOutput, calls=%fused_computation.1 | convolution fusion | flops 68811008 | bytes 5294080 | tf_op jit(solution)/shard_map/dot_general | solution.py:50
  98.2 6.8 %psum.53 = f32[512]{0:T(512)} all-reduce(f32[512]{0:T(512)} %get-tuple-element.5), channel_id=1, replica_groups=mesh['dp'=8,'tensor'=4] {'tensor'}, use_global_device_ids=true, to_apply=%region_12.13 | all-reduce | flops 512 | bytes 4096 | tf_op jit(solution)/shard_map/psum | solution.py:51
  105.0 0.7 fusion.8
  105.7 3.5 subtract_convert_fusion
  109.2 0.0 all-gather.2.cloned.1.call-update
  109.2 0.2 reduce-scatter.5.cloned.1.call-start
  109.5 40.8 %all-gather.2.cloned.1.call-done = bf16[512,5120]{1,0:T(8,128)(2,1)} async-done(((bf16[512,1280]{1,0:T(8,128)(2,1)}), bf16[512,5120]{1,0:T(8,128)(2,1)}) %all-gather.2.cloned.1.call-update) | async-done | bytes 5242896 | tf_op jit(solution)/shard_map/all_gather | solution.py:61
  150.2 11.4 %fusion.16 = f32[5120,640]{1,0:T(8,128)} fusion(bf16[512,5120]{1,0:T(8,128)(2,1)} %all-gather.2.cloned.1.call-done, bf16[512,640]{1,0:T(8,128)(2,1)S(1)} %copy-done), kind=kOutput, calls=%fused_computation.40 | convolution fusion | flops 3355443200 | bytes 19005440 | tf_op jit(solution)/shard_map/rd,rj->dj/dot_general | solution.py:59
  161.7 0.0 reduce-scatter.5.cloned.1.call-update
  161.7 0.7 copy-done.4
  162.3 2.5 fusion
  164.9 41.5 %all-reduce = (f32[8]{0:T(128)S(1)}, f32[8]{0:T(128)S(1)}, f32[1280,8]{0,1:T(8,128)}, f32[1280]{0:T(1024)}) all-reduce(f32[8]{0:T(128)} %get-tuple-element.7, f32[8]{0:T(128)} %get-tuple-element.6, f32[1280,8]{0,1:T(8,128)} %fusion, f32[1280]{0:T(1024)} %get-tuple-element.4), channel_id=1, replica_groups=mesh['dp'=8,'tensor'=4] {'dp'}, use_global_device_ids=true, to_apply=%region_8.9 | all-reduce | flops 11536 | bytes 92288 | tf_op jit(solution)/shard_map/psum | solution.py:36
  206.4 0.8 fusion.6
  207.1 0.8 multiply_reduce_fusion.3
  207.9 0.5 multiply_subtract_fusion
  208.4 169.5 %reduce-scatter.5.cloned.1.call-done = f32[640,640]{1,0:T(8,128)} async-done(((f32[5120,640]{1,0:T(8,128)}), f32[640,640]{1,0:T(8,128)}) %reduce-scatter.5.cloned.1.call-update) | async-done | bytes 1638416 | tf_op jit(solution)/shard_map/reduce_scatter | solution.py:65
  (14 shorter events, 0.1 us)
Async XLA Ops:
  7.2 1.1 copy-start
  7.2 64.0 %reduce-scatter.3.cloned.1.call-start = ((), (), s32[]{:S(2)}) async-start(), calls=%async_computation.2 | async-start | bytes 6553600 | tf_op jit(solution)/shard_map/reduce_scatter | solution.py:23
  17.1 0.7 copy-start.8
  17.1 1.5 copy-start.6
  17.1 54.1 %copy-start.1 = (bf16[512,1280]{1,0:T(8,128)(2,1)S(1)}, bf16[512,1280]{1,0:T(8,128)(2,1)}, u32[]{:S(2)}) copy-start(bf16[512,1280]{1,0:T(8,128)(2,1)} %param.7) | copy-start | bytes 3932164
  17.1 61.8 %copy-start.7 = (bf16[1280,8]{0,1:T(8,128)(2,1)S(1)}, bf16[1280,8]{0,1:T(8,128)(2,1)}, u32[]{:S(2)}) copy-start(bf16[1280,8]{0,1:T(8,128)(2,1)} %param.9) | copy-start | bytes 61444
  17.1 133.1 %all-gather.2.cloned.1.call-start = ((), (), s32[]{:S(2)}) async-start(), calls=%async_computation.3 | async-start | bytes 6553600 | tf_op jit(solution)/shard_map/all_gather | solution.py:61
  18.4 72.9 %copy-start.5 = (f32[8]{0:T(128)}, f32[8]{0:T(128)S(1)}, u32[]{:S(2)}) copy-start(f32[8]{0:T(128)S(1)} %add_convert_fusion) | copy-start | bytes 100
  71.2 7.7 %copy-start.2 = (bf16[512,1280]{1,0:T(8,128)(2,1)S(1)}, bf16[512,1280]{1,0:T(8,128)(2,1)}, u32[]{:S(2)}) copy-start(bf16[512,1280]{1,0:T(8,128)(2,1)} %reduce-scatter.3.cloned.1.call-done) | copy-start | bytes 3932164
  78.9 1.8 copy-start.3
  109.2 268.7 %reduce-scatter.5.cloned.1.call-start = ((), (), s32[]{:S(2)}) async-start(), calls=%async_computation.4 | async-start | bytes 14745600 | tf_op jit(solution)/shard_map/reduce_scatter | solution.py:65
  161.7 0.7 copy-start.4
Sparse Core Ops, SparseCore 0:
  17.2 53.8 reduce-scatter.2
  109.4 40.8 all-gather.1
  161.8 216.0 reduce-scatter.4
where the time goes:
time: 385 us; the launch traced here: 384 us
  waiting for transfers between devices  263 us (68%)
  blocking collectives  64.3 us (17%)
  matrix products  29.2 us (8%)
  between operations  13.8 us (4%)
  other arithmetic  9.97 us (3%)
  local copies, waits for them, and re-layouts  3.95 us (1%)
    reduce_scatter x1, waiting for transfers between devices, per_device(): proj_grad = lax.psum_scatter(term, 'dp', scatter_dimension=0, tiled=True)  170 us
    reduce_scatter x1, waiting for transfers between devices, per_device(): lax.psum_scatter(product.astype(jnp.bfloat16), 'tensor', scatter_dimensio...  52.6 us
    psum x1, blocking collectives, per_device(): lax.psum((jnp.sum(rewards, axis=0), jnp.sum(rewards * rewards, axis=0)),...  41.5 us
    all_gather x1, waiting for transfers between devices, per_device(): lax.all_gather(dhidden, 'tensor', axis=1, tiled=True)  40.8 us
    dot_general x1, matrix products, per_device(): jnp.einsum('rd,rj->dj', lax.all_gather(dhidden, 'tensor', axis=1, tiled=T...  11.4 us
    psum x1, blocking collectives, per_device(): scores = lax.psum(jnp.dot(normed, heads_local, precision=highest), 'tensor')  10.3 us
    dot_general x1, matrix products, per_device(): product = jnp.dot(attn_out, out_proj, preferred_element_type=jnp.float32)  8.81 us
  transfers between devices with their start and end apart: 3, of which 3 were waited for; matrix products, arithmetic and copies ran while one was open for 1% of the time, Pallas kernels for 0%

commit v1 on v0

v1 whole, which is shorter than its diff:
```python
import jax
import jax.numpy as jnp
from jax import lax
from jax.sharding import PartitionSpec as P


EPS_NORM = 1e-06
EPS_VAR = 1e-05
PENALTY = 0.5
LINE_LIMIT = 4


def swap(value, bit, axis="tensor"):
    return lax.ppermute(value, axis, [(i, i ^ bit) for i in range(lax.axis_size(axis))])


def gather_rows(own):
    n_dp = lax.axis_size("dp")
    line = n_dp // 2
    if line > LINE_LIMIT:
        return lax.all_gather(own, "dp", axis=0)
    d = lax.axis_index("dp")
    z, x = d // 2, d % 2

    def pair(value, first, last):
        return lax.ppermute(
            value, "dp", [(i, i ^ 1) for i in range(n_dp) if first <= i // 2 <= last]
        )

    found = jnp.zeros((n_dp,) + own.shape, own.dtype)
    found = lax.dynamic_update_index_in_dim(found, own, d, 0)
    found = lax.dynamic_update_index_in_dim(found, pair(own, 0, line - 1), d ^ 1, 0)
    up, down = own, own
    ups, downs = {}, {}
    for s in range(1, line):
        up = lax.ppermute(up, "dp", [(i, i + 2) for i in range(2 * (s - 1), n_dp - 2)])
        down = lax.ppermute(down, "dp", [(i, i - 2) for i in range(2, n_dp - 2 * (s - 1))])
        ups[s] = (up, pair(up, s, line - 1))
        downs[s] = (down, pair(down, 0, line - 1 - s))
    for s in range(1, line):
        place = 2 * ((z - s) % line)
        mine = ups[s][0] + downs[line - s][0]
        twin = ups[s][1] + downs[line - s][1]
        found = lax.dynamic_update_index_in_dim(found, mine, place + x, 0)
        found = lax.dynamic_update_index_in_dim(found, twin, place + 1 - x, 0)
    return found


def per_device(attn_out, resid, out_proj, heads, gain, lengths):
    f32, bf16 = jnp.float32, jnp.bfloat16
    rows, width = attn_out.shape
    cols = resid.shape[1]
    resp_dev = lengths.shape[0]
    seq_len = rows // resp_dev
    members = heads.shape[1]
    n_t = lax.axis_size("tensor")
    n_dp = lax.axis_size("dp")
    model = cols * n_t
    block = model // n_dp
    quarter = rows // n_t
    resp = resp_dev // n_t
    t = lax.axis_index("tensor")
    d = lax.axis_index("dp")
    low, high = t % 2, t // 2
    highest = lax.Precision.HIGHEST

    def pick(value, at, axis):
        return lax.dynamic_index_in_dim(value, at, axis, keepdims=False)

    gain_heads = jnp.concatenate([heads.astype(f32).T, gain.astype(f32)[None]], 0)
    bits = [1 << i for i in range((n_t - 1).bit_length())]
    parts = gain_heads[None]
    for bit in bits:
        parts = jnp.concatenate([parts, swap(parts, bit)], 0)
    order = [0]
    for bit in bits:
        order = order + [i ^ bit for i in order]
    where_is = jnp.array(order, jnp.int32)
    everything = jnp.concatenate([pick(parts, where_is[t ^ j], 0) for j in range(n_t)], 1)
    heads_all, gain_all = everything[:members], everything[members]

    attn_all = gather_rows(attn_out)

    a4 = attn_out.reshape(n_t // 2, 2, quarter, width)
    r4 = resid.reshape(n_t // 2, 2, quarter, cols)
    half = rows // 2
    a_keep, a_send = (pick(a4, b, 1).reshape(half, width) for b in (low, 1 - low))
    r_keep, r_send = (pick(r4, b, 1).reshape(half, cols) for b in (low, 1 - low))
    pieces = []
    for j in range(n_t):
        w = out_proj[:, j * cols:(j + 1) * cols]
        own = (t == j).astype(f32)
        send = jnp.dot(a_send, w, preferred_element_type=f32) + own * r_send.astype(f32)
        got = swap(send.astype(bf16), 1)
        keep = jnp.dot(a_keep, w, preferred_element_type=f32) + own * r_keep.astype(f32)
        pair = (keep + got.astype(f32)).reshape(n_t // 2, quarter, cols)
        got = swap(pick(pair, 1 - high, 0).astype(bf16), 2)
        pieces.append(pick(pair, high, 0) + got.astype(f32))
    hidden = jnp.concatenate(pieces, 1)
    full = hidden.astype(bf16).reshape(quarter, n_dp, block).transpose(1, 0, 2)
    moved = lax.all_to_all(full, "dp", 0, 0, tiled=True)
    arrived = {0: moved}
    arrived[2] = swap(moved, 2)
    arrived[1] = swap(moved, 1)
    arrived[3] = swap(arrived[2], 1)

    squares = jnp.sum(hidden * hidden, axis=1)
    raw = lax.dot_general(
        heads_all * gain_all[None, :], hidden, (((1,), (1,)), ((), ())), precision=highest
    )
    rinv = lax.rsqrt(squares / model + EPS_NORM)
    scores = raw * rinv[None, :]
    length = lax.dynamic_slice_in_dim(lengths, t * resp, resp)
    position = lax.broadcasted_iota(jnp.int32, (resp, seq_len), 1)
    inside = position <= length[:, None]
    counts = (length + 1).astype(f32)
    per_resp = scores.reshape(members, resp, seq_len)
    rewards = jnp.sum(jnp.where(inside[None], per_resp, 0.0), axis=2) / counts[None, :]
    pairs = rewards.reshape(members, resp // 2, 2)
    weight = jax.nn.sigmoid(pairs[:, :, 1] - pairs[:, :, 0])
    dreward = jnp.stack([-weight, weight], axis=2).reshape(members, resp)
    dscore = jnp.where(inside[None], (dreward / counts[None, :])[:, :, None], 0.0).reshape(
        members, quarter
    )
    inner = jnp.sum(dscore * raw, axis=0)
    coef = rinv**3 * inner / model
    lead = dscore * rinv[None, :]
    h_term = jnp.dot(lead, hidden, precision=highest)

    spread_rewards = jnp.pad(rewards, ((0, 0), (0, quarter - resp)))
    small = jnp.concatenate([lead, spread_rewards, coef[None]], 0)[None]
    for bit in bits:
        small = jnp.concatenate([small, swap(small, bit)], 0)
    t_index = jnp.array(order, jnp.int32)
    small = jnp.stack([pick(small, t_index[t ^ j], 0) for j in range(n_t)], 0)[None]
    dp_bits = [1 << i for i in range((n_dp - 1).bit_length())]
    dp_order = [0]
    for bit in dp_bits:
        small = jnp.concatenate([small, swap(small, bit, "dp")], 0)
        dp_order = dp_order + [i ^ bit for i in dp_order]
    dp_index = jnp.array(dp_order, jnp.int32)
    small = jnp.take(small, dp_index[jnp.arange(n_dp) ^ d], axis=0)
    lead_all = small[:, :, :members]
    rewards_all = small[:, :, members:2 * members, :resp]
    coef_all = small[:, :, 2 * members]

    h_sum = h_term.reshape(members, n_t // 2, 2, cols)
    h_sum = pick(h_sum, low, 2) + swap(pick(h_sum, 1 - low, 2), 1)
    h_sum = pick(h_sum, high, 1) + swap(pick(h_sum, 1 - high, 1), 2)
    for bit in dp_bits:
        h_sum = h_sum + swap(h_sum, bit, "dp")
    head_grad = (gain.astype(f32)[None, :] * h_sum).T
    gain_grad = jnp.sum(heads.astype(f32).T * h_sum, axis=0)

    center = jnp.mean(rewards_all, axis=(0, 1, 3))
    spread = jnp.mean((rewards_all - center[None, None, :, None]) ** 2, axis=(0, 1, 3))
    own_rewards = pick(rewards_all, d, 0)
    zed = (own_rewards - center[None, :, None]) * lax.rsqrt(spread + EPS_VAR)[None, :, None]
    zmean = jnp.mean(zed, axis=1)
    uwo = zmean - PENALTY * jnp.mean((zed - zmean[:, None, :]) ** 2, axis=1)
    uwo = uwo.reshape(resp_dev)

    lead_all = lead_all.transpose(2, 0, 1, 3).reshape(members, n_dp * rows)
    lead_hi = lead_all.astype(bf16)
    lead_lo = (lead_all - lead_hi.astype(f32)).astype(bf16)
    m2 = jnp.dot(
        jnp.concatenate([lead_hi, lead_lo], 0),
        attn_all.reshape(n_dp * rows, width),
        preferred_element_type=f32,
    )
    m = m2[:members] + m2[members:]
    gh_mine = lax.dynamic_slice_in_dim(heads_all * gain_all[None, :], d * block, block, 1)
    total = lax.dot_general(gh_mine, m, (((0,), (0,)), ((), ())), precision=highest)
    attn5 = attn_all.reshape(n_dp, n_t, quarter, width)
    for away in (0, 2, 1, 3):
        other = pick(attn5, t ^ away, 1).astype(f32) * pick(coef_all, t ^ away, 1)[:, :, None]
        total = total - lax.dot_general(
            arrived[away].reshape(n_dp * quarter, block),
            other.astype(bf16).reshape(n_dp * quarter, width),
            (((0,), (0,)), ((), ())),
            preferred_element_type=f32,
        )
    return (uwo, total, head_grad, gain_grad)


def solution(mesh):
    return jax.shard_map(
        per_device,
        mesh=mesh,
        in_specs=(
            P("dp", "tensor"),
            P("dp", "tensor"),
            P("tensor", None),
            P("tensor", None),
            P("tensor"),
            P("dp"),
        ),
        out_specs=(P("dp"), P("dp", "tensor"), P("tensor", None), P("tensor")),
        check_vma=False,
    )
```

time: 385 us -> 227 us (0.59)
  waiting for transfers between devices: 263 us -> 94.1 us
  blocking collectives: 64.3 us -> 0 us
  starting transfers between devices: 0.3 us -> 50.3 us
  other arithmetic: 9.97 us -> 24.7 us
  matrix products: 29.2 us -> 41.9 us
  between operations: 13.8 us -> 1.34 us
  local copies, waits for them, and re-layouts: 3.95 us -> 13.7 us
    reduce_scatter x2 -> x0, waiting for transfers between devices: 222 us -> none  [the longest x1 170 us: per_device(): proj_grad = lax.psum_scatter(term, 'dp', scatter_dimension=0, tiled=True)]
    ppermute x0 -> x36, waiting for transfers between devices: none -> 94.1 us  [the longest x23 61.9 us: swap(): lax.ppermute(value, axis, [(i, i ^ bit) for i in range(lax.axis_size(axis...]
    psum x4 -> x0, blocking collectives: 64.3 us -> none  [the longest x1 41.5 us: per_device(): lax.psum((jnp.sum(rewards, axis=0), jnp.sum(rewards * rewards, axis=0)),...]
    ppermute x0 -> x36, starting transfers between devices: none -> 45.7 us  [the longest x23 17.2 us: swap(): lax.ppermute(value, axis, [(i, i ^ bit) for i in range(lax.axis_size(axis...]
    all_gather x1 -> x0, waiting for transfers between devices: 40.8 us -> none  [per_device(): lax.all_gather(dhidden, 'tensor', axis=1, tiled=True)]
    dynamic_update_slice x0 -> x6, other arithmetic: none -> 13.2 us  [the longest x3 6.7 us: gather_rows(): found = lax.dynamic_update_index_in_dim(found, twin, place + 1 - x, 0)]
    dot_general x5 -> x16, matrix products: 29.2 us -> 41.9 us  [the longest x4 12.4 us: per_device(): jnp.dot(a_send, w, preferred_element_type=f32) + own * r_send.astype(f32)]
    all_to_all x0 -> x1, starting transfers between devices: none -> 4.58 us  [per_device(): moved = lax.all_to_all(full, 'dp', 0, 0, tiled=True)]
  transfers between devices with their start and end apart: 3 -> 37, of which waited for: 3 -> 15; matrix products, arithmetic and copies ran while one was open for 1% -> 33% of each run, Pallas kernels for 0% -> 0%
where the time goes in v1:
time: 227 us; the launch traced here: 226 us
  waiting for transfers between devices  94.1 us (41%)
  starting transfers between devices  50.3 us (22%)
  matrix products  41.9 us (18%)
  other arithmetic  24.7 us (11%)
  local copies, waits for them, and re-layouts  13.7 us (6%)
    ppermute x23, waiting for transfers between devices, swap(): lax.ppermute(value, axis, [(i, i ^ bit) for i in range(lax.axis_size(axis...  61.9 us
    ppermute x7, waiting for transfers between devices, pair(): lax.ppermute(value, 'dp', [(i, i ^ 1) for i in range(n_dp) if first <= i...  18.1 us
    ppermute x23, starting transfers between devices, swap(): lax.ppermute(value, axis, [(i, i ^ bit) for i in range(lax.axis_size(axis...  17.2 us
    ppermute x7, starting transfers between devices, pair(): lax.ppermute(value, 'dp', [(i, i ^ 1) for i in range(n_dp) if first <= i...  16.9 us
    ppermute x3, waiting for transfers between devices, gather_rows(): lax.ppermute(down, 'dp', [(i, i - 2) for i in range(2, n_dp - 2 * (s - 1))])  14.1 us
    dot_general x4, matrix products, per_device(): jnp.dot(a_send, w, preferred_element_type=f32) + own * r_send.astype(f32)  12.4 us
    dot_general x4, matrix products, per_device(): lax.dot_general(arrived[away].reshape(n_dp * quarter, block), other.astyp...  11.8 us
    ppermute x3, starting transfers between devices, gather_rows(): lax.ppermute(up, 'dp', [(i, i + 2) for i in range(2 * (s - 1), n_dp - 2)])  7.61 us
  transfers between devices with their start and end apart: 37, of which 15 were waited for; matrix products, arithmetic and copies ran while one was open for 33% of the time, Pallas kernels for 0%

profile of v1, /device:TPU:0, one launch (start us, length us, event | category | flops | bytes accessed | tf_op | source)
XLA Modules:
  0.0 226.1 jit_solution(15379375459621125666)
XLA Ops:
  0.6 3.0 %collective-permute-start.15 = (bf16[512,640]{1,0:T(8,128)(2,1)}, bf16[512,640]{1,0:T(8,128)(2,1)}, u32[]{:S(2)}, u32[]{:S(2)}) collective-permute-start(bf16[512,640]{1,0:T(8,128)(2,1)} %param.9), channel_id=1, source_target_pairs={{0,4},{4,0},{8,12},{12,8},{16,20},{20,16},{24,28},{28,24},{1,5},{5... | collective-permute-start | bytes 1966088 | tf_op jit(solution)/shard_map/ppermute | solution.py:26
  5.0 5.4 %collective-permute-start.16 = (bf16[512,640]{1,0:T(8,128)(2,1)}, bf16[512,640]{1,0:T(8,128)(2,1)}, u32[]{:S(2)}, u32[]{:S(2)}) collective-permute-start(bf16[512,640]{1,0:T(8,128)(2,1)} %param.9), channel_id=1, source_target_pairs={{0,8},{4,12},{8,16},{12,20},{16,24},{20,28},{1,9},{5,13},{9,17},{1... | collective-permute-start | bytes 1966088 | tf_op jit(solution)/shard_map/ppermute | solution.py:36
  11.9 3.4 %convert_multiply_fusion.7 = (f32[2,1,128,1280]{3,2,0,1:T(8,128)S(1)}, f32[2,1,128,1280]{3,2,0,1:T(8,128)}, f32[2,1,128,1280]{3,2,0,1:T(8,128)}, f32[2,1,128,128...) fusion(f32[]{:T(128)S(6)} %convert_element_type.145, ...), kind=kLoop, calls=%fused_computation.27 | loop fusion | flops 3276800 | bytes 11796504 | tf_op jit(solution)/shard_map/mul | solution.py:93
  15.3 3.0 %fusion.4 = bf16[256,1280]{1,0:T(8,128)(2,1)} fusion(f32[256,1280]{1,0:T(8,128)S(1)} %bitcast.211, bf16[256,640]{1,0:T(8,128)(2,1)S(1)} %bitcast.200, bf16[640,5120]{1,0:T(8,128)(2,1)} %param.11), kind=kOutput, calls=%fused_computation.20 | convolution fusion | flops 420085760 | bytes 3932160 | tf_op jit(solution)/shard_map/dot_general | solution.py:93
  20.1 3.5 %fusion.5 = bf16[256,1280]{1,0:T(8,128)(2,1)} fusion(f32[256,1280]{1,0:T(8,128)} %bitcast.210, bf16[256,640]{1,0:T(8,128)(2,1)S(1)} %bitcast.201, bf16[640,5120]{1,0:T(8,128)(2,1)} %param.11), kind=kOutput, calls=%fused_computation.21 | convolution fusion | flops 420085760 | bytes 3932160 | tf_op jit(solution)/shard_map/dot_general | solution.py:93
  23.6 3.0 %fusion.6 = bf16[256,1280]{1,0:T(8,128)(2,1)} fusion(f32[256,1280]{1,0:T(8,128)S(1)} %bitcast.209, bf16[256,640]{1,0:T(8,128)(2,1)S(1)} %bitcast.202, bf16[640,5120]{1,0:T(8,128)(2,1)} %param.11), kind=kOutput, calls=%fused_computation.22 | convolution fusion | flops 420085760 | bytes 3932160 | tf_op jit(solution)/shard_map/dot_general | solution.py:93
  26.6 3.0 %fusion.7 = bf16[256,1280]{1,0:T(8,128)(2,1)} fusion(f32[256,1280]{1,0:T(8,128)S(1)} %bitcast.208, bf16[256,640]{1,0:T(8,128)(2,1)S(1)} %bitcast.203, bf16[640,5120]{1,0:T(8,128)(2,1)} %param.11), kind=kOutput, calls=%fused_computation.23 | convolution fusion | flops 420085760 | bytes 3932160 | tf_op jit(solution)/shard_map/dot_general | solution.py:93
  29.6 2.7 %broadcast_in_dim.115 = bf16[8,512,640]{2,1,0:T(8,128)(2,1)} broadcast(bf16[]{:T(256)} %constant.230.clone.1), dimensions={} | broadcast | bytes 5242882 | tf_op jit(solution)/shard_map/broadcast_in_dim | solution.py:30
  33.7 1.6 collective-permute-start.1
  35.3 4.6 %collective-permute-done.1 = f32[2,9,1280]{2,1,0:T(8,128)S(1)} collective-permute-done((f32[2,9,1280]{2,1,0:T(8,128)S(1)}, f32[2,9,1280]{2,1,0:T(8,128)S(1)}, u32[]{:S(2)}, u32[]{:S(2)}) %collective-permute-start.1) | collective-permute-done | bytes 92192 | tf_op jit(solution)/shard_map/ppermute | solution.py:14
  40.6 2.4 %convert_add_fusion.3 = f32[256,1280]{1,0:T(8,128)S(1)} fusion(bf16[256,1280]{1,0:T(8,128)(2,1)} %collective-permute-done.2, f32[256,1280]{1,0:T(8,128)S(1)} %bitcast.207, bf16[256,640]{1,0:T(8,128)(2,1)S(1)} %bitcast.196, bf16[640,5120]{1,0:T(8,128)(2,1)} %param.11), kind=kOutput, calls=%fused_computation.63 | convolution fusion | flops 420413440 | bytes 5242880 | tf_op jit(solution)/shard_map/dot_general | solution.py:95
  44.0 1.6 collective-permute-start.3
  47.7 1.6 collective-permute-start.7
  49.3 2.0 bitcast_dynamic-update-slice_fusion.6
  51.9 2.7 %collective-permute-done.3 = bf16[128,1280]{1,0:T(8,128)(2,1)S(1)} collective-permute-done((bf16[128,1280]{1,0:T(8,128)(2,1)S(1)}, bf16[128,1280]{1,0:T(8,128)(2,1)S(1)}, u32[]{:S(2)}, u32[]{:S(2)}) %collective-permute-start.3) | collective-permute-done | bytes 327712 | tf_op jit(solution)/shard_map/ppermute | solution.py:14
  58.4 3.3 %collective-permute-done.5 = bf16[128,1280]{1,0:T(8,128)(2,1)S(1)} collective-permute-done((bf16[128,1280]{1,0:T(8,128)(2,1)S(1)}, bf16[128,1280]{1,0:T(8,128)(2,1)S(1)}, u32[]{:S(2)}, u32[]{:S(2)}) %collective-permute-start.5) | collective-permute-done | bytes 327712 | tf_op jit(solution)/shard_map/ppermute | solution.py:14
  64.0 4.7 %collective-permute-done.7 = bf16[128,1280]{1,0:T(8,128)(2,1)S(1)} collective-permute-done((bf16[128,1280]{1,0:T(8,128)(2,1)S(1)}, bf16[128,1280]{1,0:T(8,128)(2,1)S(1)}, u32[]{:S(2)}, u32[]{:S(2)}) %collective-permute-start.7) | collective-permute-done | bytes 327712 | tf_op jit(solution)/shard_map/ppermute | solution.py:14
  69.5 5.7 %collective-permute-done.9 = bf16[128,1280]{1,0:T(8,128)(2,1)S(1)} collective-permute-done((bf16[128,1280]{1,0:T(8,128)(2,1)S(1)}, bf16[128,1280]{1,0:T(8,128)(2,1)S(1)}, u32[]{:S(2)}, u32[]{:S(2)}) %collective-permute-start.9) | collective-permute-done | bytes 327712 | tf_op jit(solution)/shard_map/ppermute | solution.py:14
  77.0 3.6 %broadcast_multiply_fusion = (f32[8,128]{1,0:T(8,128)S(1)}, f32[8,128]{1,0:T(8,128)S(1)}) fusion(f32[128]{0:T(128)S(1)} %add_rsqrt_fusion.1, f32[8,5120]{1,0:T(8,128)S(1)} %slice_multiply_fusion, f32[128,1280]{1,0:T(8,128)} %copy-done.8, f32[128,1280]{1,0:T(8,128)} %copy-done.7, f32[128,1280]{1,0:T(8,128)} %copy-done.6, f32[128,1280]{1,0:T(8,128)S(1)} %get-tuple-element.7), kind=kOutput, calls=%fused_computation.159 | convolution fusion | flops 64881664 | bytes 2793984 | tf_op jit(solution)/shard_map/dot_general | solution.py:108
  81.2 2.2 copy.45
  83.7 4.0 %fusion.56 = f32[8,2,2,1280]{3,0,2,1:T(8,128)S(1)} fusion(f32[2,2,1280,128]{3,2,1,0:T(8,128)} %bitcast.195, f32[8,128,1,1]{1,0,2,3:T(8,128)S(1)} %reshape.389), kind=kOutput, calls=%fused_computation.146 | convolution fusion | flops 62914560 | bytes 2789376 | tf_op jit(solution)/shard_map/dot_general | solution.py:128
  87.7 1.6 collective-permute-start.11
  91.7 1.6 collective-permute-start.32
  93.8 1.9 collective-permute-done.32
  101.9 4.6 %all-to-all-start = ((bf16[8,128,640]{1,2,0:T(8,128)(2,1)}), bf16[8,128,640]{1,2,0:T(8,128)(2,1)S(1)}, u32[]{:S(2)}, u32[]{:S(2)}) async-start(bf16[8,128,640]{1,2,0:T(8,128)(2,1)} %maximum_bitcast_fusion), calls=%async_computation | async-start | bytes 2621440 | tf_op jit(solution)/shard_map/all_to_all | solution.py:101
  106.5 3.0 %collective-permute-start.35 = (f32[8,1280]{1,0:T(8,128)S(1)}, f32[8,1280]{1,0:T(8,128)S(1)}, u32[]{:S(2)}, u32[]{:S(2)}) collective-permute-start(f32[8,1280]{1,0:T(8,128)S(1)} %add.374), channel_id=1, source_target_pairs={{0,16},{4,20},{8,24},{12,28},{16,0},{20,4},{24,8},{28,12},{1,17},{... | collective-permute-start | bytes 122888 | tf_op jit(solution)/shard_map/ppermute | solution.py:14
  109.6 34.0 %collective-permute-done.35 = f32[8,1280]{1,0:T(8,128)S(1)} collective-permute-done((f32[8,1280]{1,0:T(8,128)S(1)}, f32[8,1280]{1,0:T(8,128)S(1)}, u32[]{:S(2)}, u32[]{:S(2)}) %collective-permute-start.35) | collective-permute-done | bytes 40992 | tf_op jit(solution)/shard_map/ppermute | solution.py:14
  149.0 14.1 %collective-permute-done.19 = bf16[512,640]{1,0:T(8,128)(2,1)S(1)} collective-permute-done((bf16[512,640]{1,0:T(8,128)(2,1)}, bf16[512,640]{1,0:T(8,128)(2,1)S(1)}, u32[]{:S(2)}, u32[]{:S(2)}) %collective-permute-start.19) | collective-permute-done | bytes 655392 | tf_op jit(solution)/shard_map/ppermute | solution.py:37
  163.1 3.5 %collective-permute-start.21 = (bf16[512,640]{1,0:T(8,128)(2,1)S(1)}, bf16[512,640]{1,0:T(8,128)(2,1)}, u32[]{:S(2)}, u32[]{:S(2)}) collective-permute-start(bf16[512,640]{1,0:T(8,128)(2,1)S(1)} %collective-permute-done.19), channel_id=1, source_target_pairs={{0,4},{4,0},{1,5},{5,1},{2,6},{6,2},{3,7},{7,3}} | collective-permute-start | bytes 1966088 | tf_op jit(solution)/shard_map/ppermute | solution.py:26
  167.6 1.5 collective-permute-start.23
  169.1 2.3 %collective-permute-start.24 = (bf16[512,640]{1,0:T(8,128)(2,1)}, bf16[512,640]{1,0:T(8,128)(2,1)}, u32[]{:S(2)}, u32[]{:S(2)}) collective-permute-start(bf16[512,640]{1,0:T(8,128)(2,1)} %collective-permute-done.18), channel_id=1, source_target_pairs={{0,4},{4,0},{8,12},{12,8},{1,5},{5,1},{9,13},{13,9},{2,6},{6,2},{1... | collective-permute-start | bytes 1966088 | tf_op jit(solution)/shard_map/ppermute | solution.py:26
  171.4 2.1 bitcast_dynamic-update-slice_fusion.5
  173.5 3.5 %collective-permute-start.27 = (bf16[512,640]{1,0:T(8,128)(2,1)}, bf16[512,640]{1,0:T(8,128)(2,1)S(1)}, u32[]{:S(2)}, u32[]{:S(2)}) collective-permute-start(bf16[512,640]{1,0:T(8,128)(2,1)} %collective-permute-done.17), channel_id=1, source_target_pairs={{0,4},{4,0},{8,12},{12,8},{16,20},{20,16},{1,5},{5,1},{9,13},{13,9... | collective-permute-start | bytes 1966088 | tf_op jit(solution)/shard_map/ppermute | solution.py:26
  177.0 1.5 collective-permute-start.26
  178.6 4.2 %collective-permute-done.21 = bf16[512,640]{1,0:T(8,128)(2,1)} collective-permute-done((bf16[512,640]{1,0:T(8,128)(2,1)S(1)}, bf16[512,640]{1,0:T(8,128)(2,1)}, u32[]{:S(2)}, u32[]{:S(2)}) %collective-permute-start.21) | collective-permute-done | bytes 655392 | tf_op jit(solution)/shard_map/ppermute | solution.py:26
  183.8 2.3 %bitcast_dynamic-update-slice_fusion.4 = bf16[8,512,640]{2,1,0:T(8,128)(2,1)} fusion(bf16[8,512,640]{2,1,0:T(8,128)(2,1)} %bitcast_dynamic-update-slice_fusion.5, s32[]{:T(128)S(6)} %select_n.224, bf16[512,640]{1,0:T(8,128)(2,1)} %collective-permute-done.20, bf16[512,640]{1,0:T(8,128)(2,1)} %collective-permute-done.21), kind=kLoop, calls=%fused_computation.68 | loop fusion | flops 1310720 | bytes 1966084 | tf_op jit(solution)/shard_map/jit(dynamic_update_index_in_dim)/dynamic_update_slice | solution.py:45
  186.1 2.3 %bitcast_dynamic-update-slice_fusion.3 = bf16[8,512,640]{2,1,0:T(8,128)(2,1)} fusion(bf16[8,512,640]{2,1,0:T(8,128)(2,1)} %bitcast_dynamic-update-slice_fusion.4, s32[]{:T(128)S(6)} %select_n.226, bf16[512,640]{1,0:T(8,128)(2,1)} %collective-permute-done.22, bf16[512,640]{1,0:T(8,128)(2,1)} %collective-permute-done.18), kind=kLoop, calls=%fused_computation.67 | loop fusion | flops 1310720 | bytes 1966084 | tf_op jit(solution)/shard_map/jit(dynamic_update_index_in_dim)/dynamic_update_slice | solution.py:44
  188.4 8.4 %collective-permute-done.24 = bf16[512,640]{1,0:T(8,128)(2,1)} collective-permute-done((bf16[512,640]{1,0:T(8,128)(2,1)}, bf16[512,640]{1,0:T(8,128)(2,1)}, u32[]{:S(2)}, u32[]{:S(2)}) %collective-permute-start.24) | collective-permute-done | bytes 655392 | tf_op jit(solution)/shard_map/ppermute | solution.py:26
  196.8 2.3 %bitcast_dynamic-update-slice_fusion.2 = bf16[8,512,640]{2,1,0:T(8,128)(2,1)} fusion(bf16[8,512,640]{2,1,0:T(8,128)(2,1)} %bitcast_dynamic-update-slice_fusion.3, s32[]{:T(128)S(6)} %select_n.227, bf16[512,640]{1,0:T(8,128)(2,1)} %collective-permute-done.23, bf16[512,640]{1,0:T(8,128)(2,1)} %collective-permute-done.24), kind=kLoop, calls=%fused_computation.66 | loop fusion | flops 1310720 | bytes 1966084 | tf_op jit(solution)/shard_map/jit(dynamic_update_index_in_dim)/dynamic_update_slice | solution.py:45
  199.1 2.1 bitcast_dynamic-update-slice_fusion.1
  201.2 5.5 %collective-permute-done.27 = bf16[512,640]{1,0:T(8,128)(2,1)S(1)} collective-permute-done((bf16[512,640]{1,0:T(8,128)(2,1)}, bf16[512,640]{1,0:T(8,128)(2,1)S(1)}, u32[]{:S(2)}, u32[]{:S(2)}) %collective-permute-start.27) | collective-permute-done | bytes 655392 | tf_op jit(solution)/shard_map/ppermute | solution.py:26
  206.6 2.1 bitcast_dynamic-update-slice_fusion
  208.7 3.3 %fusion.41 = f32[16,640]{1,0:T(8,128)S(1)} fusion(bf16[4096,640]{1,0:T(8,128)(2,1)} %bitcast.52, bf16[8,4096]{1,0:T(8,128)(2,1)S(1)} %get-tuple-element.4, bf16[8,4096]{1,0:T(8,128)(2,1)S(1)} %get-tuple-element.5), kind=kOutput, calls=%fused_computation.93 | convolution fusion | flops 84148224 | bytes 5414912 | tf_op jit(solution)/shard_map/dot_general | solution.py:166
  212.0 2.2 fusion.45
  214.3 2.6 %fusion.16 = f32[640,640,1]{1,0,2:T(8,128)S(1)} fusion(bf16[8,128,640]{1,2,0:T(8,128)(2,1)S(1)} %all-to-all-done, f32[8,128]{1,0:T(8,128)S(1)} %bitcast.231, bf16[8,4,128,640]{3,2,1,0:T(8,128)(2,1)} %bitcast.58, s32[]{:T(128)S(6)} %select_n.195), kind=kOutput, calls=%fused_computation.44 | convolution fusion | flops 840826880 | bytes 4263940 | tf_op jit(solution)/shard_map/dot_general | solution.py:177
  216.9 2.6 %fusion.18 = f32[640,640,1]{1,0,2:T(8,128)S(1)} fusion(bf16[8,128,640]{1,2,0:T(8,128)(2,1)S(1)} %collective-permute-done.28, f32[8,128]{1,0:T(8,128)S(1)} %bitcast.230, bf16[8,4,128,640]{3,2,1,0:T(8,128)(2,1)} %bitcast.58, s32[]{:T(128)S(6)} %select_n.199), kind=kOutput, calls=%fused_computation.45 | convolution fusion | flops 840826880 | bytes 4263940 | tf_op jit(solution)/shard_map/dot_general | solution.py:177
  219.6 2.7 %fusion.20 = f32[640,640,1]{1,0,2:T(8,128)S(1)} fusion(bf16[8,128,640]{1,2,0:T(8,128)(2,1)S(1)} %collective-permute-done.29, f32[8,128]{1,0:T(8,128)S(1)} %bitcast.229, bf16[8,4,128,640]{3,2,1,0:T(8,128)(2,1)} %bitcast.58, s32[]{:T(128)S(6)} %select_n.197), kind=kOutput, calls=%fused_computation.46 | convolution fusion | flops 840826880 | bytes 4263940 | tf_op jit(solution)/shard_map/dot_general | solution.py:177
  222.2 3.8 %bitcast_subtract_fusion = f32[640,640]{1,0:T(8,128)} fusion(f32[640,640,1]{1,0,2:T(8,128)S(1)} %fusion.20, f32[640,640,1]{1,0,2:T(8,128)S(1)} %fusion.18, f32[640,640]{1,0:T(8,128)S(1)} %fusion.45, f32[640,640,1]{1,0,2:T(8,128)S(1)} %fusion.16, bf16[8,128,640]{1,2,0:T(8,128)(2,1)S(1)} %collective-permute-done.30, f32[8,128]{1,0:T(8,128)S(1)} %bitcast.228, ...), kind=kOutput, calls=%fused_computation.32 | convolution fusion | flops 842465280 | bytes 10817540 | tf_op jit(solution)/shard_map/dot_general | solution.py:177
  (188 shorter events, 36.1 us)
Async XLA Ops:
  0.6 47.1 %collective-permute-start.15 = (bf16[512,640]{1,0:T(8,128)(2,1)}, bf16[512,640]{1,0:T(8,128)(2,1)}, u32[]{:S(2)}, u32[]{:S(2)}) collective-permute-start(bf16[512,640]{1,0:T(8,128)(2,1)} %param.9), channel_id=1, source_target_pairs={{0,4},{4,0},{8,12},{12,8},{16,20},{20,16},{24,28},{28,24},{1,5},{5... | collective-permute-start | bytes 1966088 | tf_op jit(solution)/shard_map/ppermute | solution.py:26
  3.7 53.3 %collective-permute-start.17 = (bf16[512,640]{1,0:T(8,128)(2,1)}, bf16[512,640]{1,0:T(8,128)(2,1)}, u32[]{:S(2)}, u32[]{:S(2)}) collective-permute-start(bf16[512,640]{1,0:T(8,128)(2,1)} %param.9), channel_id=1, source_target_pairs={{8,0},{12,4},{16,8},{20,12},{24,16},{28,20},{9,1},{13,5},{17,9},{2... | collective-permute-start | bytes 1966088 | tf_op jit(solution)/shard_map/ppermute | solution.py:37
  5.0 46.4 %collective-permute-start.16 = (bf16[512,640]{1,0:T(8,128)(2,1)}, bf16[512,640]{1,0:T(8,128)(2,1)}, u32[]{:S(2)}, u32[]{:S(2)}) collective-permute-start(bf16[512,640]{1,0:T(8,128)(2,1)} %param.9), channel_id=1, source_target_pairs={{0,8},{4,12},{8,16},{12,20},{16,24},{20,28},{1,9},{5,13},{9,17},{1... | collective-permute-start | bytes 1966088 | tf_op jit(solution)/shard_map/ppermute | solution.py:36
  18.3 21.8 %collective-permute-start.2 = (bf16[256,1280]{1,0:T(8,128)(2,1)}, bf16[256,1280]{1,0:T(8,128)(2,1)}, u32[]{:S(2)}, u32[]{:S(2)}) collective-permute-start(bf16[256,1280]{1,0:T(8,128)(2,1)} %fusion.4), channel_id=1, source_target_pairs={{0,1},{1,0},{2,3},{3,2},{4,5},{5,4},{6,7},{7,6},{8,9},{9,8},{10,11... | collective-permute-start | bytes 1966088 | tf_op jit(solution)/shard_map/ppermute | solution.py:14
  18.3 15.3 %collective-permute-start = (f32[1,9,1280]{2,1,0:T(8,128)S(1)}, f32[1,9,1280]{2,1,0:T(8,128)S(1)}, u32[]{:S(2)}, u32[]{:S(2)}) collective-permute-start(f32[1,9,1280]{2,1,0:T(8,128)S(1)} %maximum_bitcast_fusion.1), channel_id=1, source_target_pairs={{0,1},{1,0},{2,3},{3,2},{4,5},{5,4},{6,7},{7,6},{8,9},{9,8},{10,11... | collective-permute-start | bytes 138248 | tf_op jit(solution)/shard_map/ppermute | solution.py:14
  20.1 3.5 %copy-start.4 = (f32[2,1,128,1280]{3,2,0,1:T(8,128)S(1)}, f32[2,1,128,1280]{3,2,0,1:T(8,128)}, u32[]{:S(2)}) copy-start(f32[2,1,128,1280]{3,2,0,1:T(8,128)} %get-tuple-element.25) | copy-start | bytes 3932164
  29.6 13.6 %slice-start = ((s8[6553600]{0:T(1024)(128)(4,1)}), s8[2359296]{0:T(1024)(128)(4,1)S(1)}, s32[]{:S(2)}) async-start(s8[6553600]{0:T(1024)(128)(4,1)} %bitcast.193), calls=%async_computation.1 | async-start | bytes 4718592
  33.6 6.4 %copy-start.15 = (bf16[256,1280]{1,0:T(8,128)(2,1)S(1)}, bf16[256,1280]{1,0:T(8,128)(2,1)}, u32[]{:S(2)}) copy-start(bf16[256,1280]{1,0:T(8,128)(2,1)} %fusion.6) | copy-start | bytes 1966084
  33.7 6.2 %collective-permute-start.1 = (f32[2,9,1280]{2,1,0:T(8,128)S(1)}, f32[2,9,1280]{2,1,0:T(8,128)S(1)}, u32[]{:S(2)}, u32[]{:S(2)}) collective-permute-start(f32[2,9,1280]{2,1,0:T(8,128)S(1)} %pad_maximum_fusion.6), channel_id=1, source_target_pairs={{0,2},{1,3},{2,0},{3,1},{4,6},{5,7},{6,4},{7,5},{8,10},{9,11},{10,... | collective-permute-start | bytes 276488 | tf_op jit(solution)/shard_map/ppermute | solution.py:14
  35.2 5.4 %copy-start.3 = (f32[2,1,128,1280]{3,2,0,1:T(8,128)S(1)}, f32[2,1,128,1280]{3,2,0,1:T(8,128)}, u32[]{:S(2)}) copy-start(f32[2,1,128,1280]{3,2,0,1:T(8,128)} %get-tuple-element.27) | copy-start | bytes 3932164
  35.3 8.0 %slice-start.1 = ((s8[6553600]{0:T(1024)(128)(4,1)}), s8[4194304]{0:T(1024)(128)(4,1)S(1)}, s32[]{:S(2)}) async-start(s8[6553600]{0:T(1024)(128)(4,1)} %bitcast.193), calls=%async_computation.2 | async-start | bytes 8388608
  39.9 3.2 %collective-permute-start.4 = (bf16[256,1280]{1,0:T(8,128)(2,1)}, bf16[256,1280]{1,0:T(8,128)(2,1)S(1)}, u32[]{:S(2)}, u32[]{:S(2)}) collective-permute-start(bf16[256,1280]{1,0:T(8,128)(2,1)} %fusion.5), channel_id=1, source_target_pairs={{0,1},{1,0},{2,3},{3,2},{4,5},{5,4},{6,7},{7,6},{8,9},{9,8},{10,11... | collective-permute-start | bytes 1966088 | tf_op jit(solution)/shard_map/ppermute | solution.py:14
  40.0 37.0 %copy-start.16 = (f32[8,5120]{1,0:T(8,128)}, f32[8,5120]{1,0:T(8,128)S(1)}, u32[]{:S(2)}) copy-start(f32[8,5120]{1,0:T(8,128)S(1)} %slice_multiply_fusion) | copy-start | bytes 491524
  40.1 3.9 %collective-permute-start.6 = (bf16[256,1280]{1,0:T(8,128)(2,1)S(1)}, bf16[256,1280]{1,0:T(8,128)(2,1)S(1)}, u32[]{:S(2)}, u32[]{:S(2)}) collective-permute-start(bf16[256,1280]{1,0:T(8,128)(2,1)S(1)} %copy-done.15), channel_id=1, source_target_pairs={{0,1},{1,0},{2,3},{3,2},{4,5},{5,4},{6,7},{7,6},{8,9},{9,8},{10,11... | collective-permute-start | bytes 1966088 | tf_op jit(solution)/shard_map/ppermute | solution.py:14
  43.1 3.3 %collective-permute-start.8 = (bf16[256,1280]{1,0:T(8,128)(2,1)S(1)}, bf16[256,1280]{1,0:T(8,128)(2,1)S(1)}, u32[]{:S(2)}, u32[]{:S(2)}) collective-permute-start(bf16[256,1280]{1,0:T(8,128)(2,1)S(1)} %copy-done.14), channel_id=1, source_target_pairs={{0,1},{1,0},{2,3},{3,2},{4,5},{5,4},{6,7},{7,6},{8,9},{9,8},{10,11... | collective-permute-start | bytes 1966088 | tf_op jit(solution)/shard_map/ppermute | solution.py:14
  44.0 10.6 %collective-permute-start.3 = (bf16[128,1280]{1,0:T(8,128)(2,1)S(1)}, bf16[128,1280]{1,0:T(8,128)(2,1)S(1)}, u32[]{:S(2)}, u32[]{:S(2)}) collective-permute-start(bf16[128,1280]{1,0:T(8,128)(2,1)S(1)} %fusion.37), channel_id=1, source_target_pairs={{0,2},{1,3},{2,0},{3,1},{4,6},{5,7},{6,4},{7,5},{8,10},{9,11},{10,... | collective-permute-start | bytes 983048 | tf_op jit(solution)/shard_map/ppermute | solution.py:14
  46.4 15.3 %collective-permute-start.5 = (bf16[128,1280]{1,0:T(8,128)(2,1)S(1)}, bf16[128,1280]{1,0:T(8,128)(2,1)S(1)}, u32[]{:S(2)}, u32[]{:S(2)}) collective-permute-start(bf16[128,1280]{1,0:T(8,128)(2,1)S(1)} %fusion.38), channel_id=1, source_target_pairs={{0,2},{1,3},{2,0},{3,1},{4,6},{5,7},{6,4},{7,5},{8,10},{9,11},{10,... | collective-permute-start | bytes 983048 | tf_op jit(solution)/shard_map/ppermute | solution.py:14
  47.7 21.0 %collective-permute-start.7 = (bf16[128,1280]{1,0:T(8,128)(2,1)S(1)}, bf16[128,1280]{1,0:T(8,128)(2,1)S(1)}, u32[]{:S(2)}, u32[]{:S(2)}) collective-permute-start(bf16[128,1280]{1,0:T(8,128)(2,1)S(1)} %fusion.39), channel_id=1, source_target_pairs={{0,2},{1,3},{2,0},{3,1},{4,6},{5,7},{6,4},{7,5},{8,10},{9,11},{10,... | collective-permute-start | bytes 983048 | tf_op jit(solution)/shard_map/ppermute | solution.py:14
  51.4 23.9 %collective-permute-start.9 = (bf16[128,1280]{1,0:T(8,128)(2,1)S(1)}, bf16[128,1280]{1,0:T(8,128)(2,1)S(1)}, u32[]{:S(2)}, u32[]{:S(2)}) collective-permute-start(bf16[128,1280]{1,0:T(8,128)(2,1)S(1)} %fusion.40), channel_id=1, source_target_pairs={{0,2},{1,3},{2,0},{3,1},{4,6},{5,7},{6,4},{7,5},{8,10},{9,11},{10,... | collective-permute-start | bytes 983048 | tf_op jit(solution)/shard_map/ppermute | solution.py:14
  54.7 118.8 %collective-permute-start.20 = (bf16[512,640]{1,0:T(8,128)(2,1)}, bf16[512,640]{1,0:T(8,128)(2,1)}, u32[]{:S(2)}, u32[]{:S(2)}) collective-permute-start(bf16[512,640]{1,0:T(8,128)(2,1)} %collective-permute-done.16), channel_id=1, source_target_pairs={{8,12},{12,8},{16,20},{20,16},{24,28},{28,24},{9,13},{13,9},{17,21... | collective-permute-start | bytes 1966088 | tf_op jit(solution)/shard_map/ppermute | solution.py:26
  56.9 91.3 %collective-permute-start.22 = (bf16[512,640]{1,0:T(8,128)(2,1)}, bf16[512,640]{1,0:T(8,128)(2,1)}, u32[]{:S(2)}, u32[]{:S(2)}) collective-permute-start(bf16[512,640]{1,0:T(8,128)(2,1)} %collective-permute-done.16), channel_id=1, source_target_pairs={{8,16},{12,20},{16,24},{20,28},{9,17},{13,21},{17,25},{21,29},{10,... | collective-permute-start | bytes 1966088 | tf_op jit(solution)/shard_map/ppermute | solution.py:36
  61.7 85.3 %collective-permute-start.18 = (bf16[512,640]{1,0:T(8,128)(2,1)}, bf16[512,640]{1,0:T(8,128)(2,1)}, u32[]{:S(2)}, u32[]{:S(2)}) collective-permute-start(bf16[512,640]{1,0:T(8,128)(2,1)} %collective-permute-done.17), channel_id=1, source_target_pairs={{8,0},{12,4},{16,8},{20,12},{9,1},{13,5},{17,9},{21,13},{10,2},{14... | collective-permute-start | bytes 1966088 | tf_op jit(solution)/shard_map/ppermute | solution.py:37
  64.0 12.6 %copy-start.6 = (f32[128,1280]{1,0:T(8,128)}, f32[128,1280]{1,0:T(8,128)S(1)}, u32[]{:S(2)}) copy-start(f32[128,1280]{1,0:T(8,128)S(1)} %get-tuple-element.9) | copy-start | bytes 1966084
  69.5 7.0 %copy-start.7 = (f32[128,1280]{1,0:T(8,128)}, f32[128,1280]{1,0:T(8,128)S(1)}, u32[]{:S(2)}) copy-start(f32[128,1280]{1,0:T(8,128)S(1)} %get-tuple-element.11) | copy-start | bytes 1966084
  83.6 4.1 %collective-permute-start.10 = (f32[1,17,128]{2,1,0:T(8,128)S(1)}, f32[1,17,128]{2,1,0:T(8,128)S(1)}, u32[]{:S(2)}, u32[]{:S(2)}) collective-permute-start(f32[1,17,128]{2,1,0:T(8,128)S(1)} %fusion.49), channel_id=1, source_target_pairs={{0,1},{1,0},{2,3},{3,2},{4,5},{5,4},{6,7},{7,6},{8,9},{9,8},{10,11... | collective-permute-start | bytes 26120 | tf_op jit(solution)/shard_map/ppermute | solution.py:14
  83.7 5.9 %copy-start.10 = (bf16[128,1280]{1,0:T(8,128)(2,1)S(1)}, bf16[128,1280]{1,0:T(8,128)(2,1)}, u32[]{:S(2)}) copy-start(bf16[128,1280]{1,0:T(8,128)(2,1)} %get-tuple-element.6) | copy-start | bytes 983044
  83.7 6.1 %copy-start.11 = (bf16[128,1280]{1,0:T(8,128)(2,1)S(1)}, bf16[128,1280]{1,0:T(8,128)(2,1)}, u32[]{:S(2)}) copy-start(bf16[128,1280]{1,0:T(8,128)(2,1)} %get-tuple-element.8) | copy-start | bytes 983044
  87.7 3.9 %collective-permute-start.11 = (f32[2,17,128]{2,1,0:T(8,128)S(1)}, f32[2,17,128]{2,1,0:T(8,128)S(1)}, u32[]{:S(2)}, u32[]{:S(2)}) collective-permute-start(f32[2,17,128]{2,1,0:T(8,128)S(1)} %pad_maximum_fusion.9), channel_id=1, source_target_pairs={{0,2},{1,3},{2,0},{3,1},{4,6},{5,7},{6,4},{7,5},{8,10},{9,11},{10,... | collective-permute-start | bytes 52232 | tf_op jit(solution)/shard_map/ppermute | solution.py:14
  89.3 2.3 %collective-permute-start.31 = (f32[8,2,1280]{2,0,1:T(8,128)S(1)}, f32[8,2,1280]{2,0,1:T(8,128)S(1)}, u32[]{:S(2)}, u32[]{:S(2)}) collective-permute-start(f32[8,2,1280]{2,0,1:T(8,128)S(1)} %dynamic-slice_bitcast_fusion), channel_id=1, source_target_pairs={{0,1},{1,0},{2,3},{3,2},{4,5},{5,4},{6,7},{7,6},{8,9},{9,8},{10,11... | collective-permute-start | bytes 245768 | tf_op jit(solution)/shard_map/ppermute | solution.py:14
  91.7 4.1 %collective-permute-start.32 = (f32[8,1280]{1,0:T(8,128)S(1)}, f32[8,1280]{1,0:T(8,128)S(1)}, u32[]{:S(2)}, u32[]{:S(2)}) collective-permute-start(f32[8,1280]{1,0:T(8,128)S(1)} %dynamic-slice_bitcast_fusion.5), channel_id=1, source_target_pairs={{0,2},{1,3},{2,0},{3,1},{4,6},{5,7},{6,4},{7,5},{8,10},{9,11},{10,... | collective-permute-start | bytes 122888 | tf_op jit(solution)/shard_map/ppermute | solution.py:14
  93.3 4.3 %collective-permute-start.12 = (f32[1,4,17,128]{3,2,1,0:T(8,128)S(1)}, f32[1,4,17,128]{3,2,1,0:T(8,128)S(1)}, u32[]{:S(2)}, u32[]{:S(2)}) collective-permute-start(f32[1,4,17,128]{3,2,1,0:T(8,128)S(1)} %maximum_bitcast_fusion.2), channel_id=1, source_target_pairs={{0,4},{4,0},{8,12},{12,8},{16,20},{20,16},{24,28},{28,24},{1,5},{5... | collective-permute-start | bytes 104456 | tf_op jit(solution)/shard_map/ppermute | solution.py:14
  95.8 4.1 %collective-permute-start.33 = (f32[8,1280]{1,0:T(8,128)S(1)}, f32[8,1280]{1,0:T(8,128)S(1)}, u32[]{:S(2)}, u32[]{:S(2)}) collective-permute-start(f32[8,1280]{1,0:T(8,128)S(1)} %bitcast_add_fusion.5), channel_id=1, source_target_pairs={{0,4},{4,0},{8,12},{12,8},{16,20},{20,16},{24,28},{28,24},{1,5},{5... | collective-permute-start | bytes 122888 | tf_op jit(solution)/shard_map/ppermute | solution.py:14
  97.6 11.8 %collective-permute-start.13 = (f32[2,4,17,128]{3,2,1,0:T(8,128)S(1)}, f32[2,4,17,128]{3,2,1,0:T(8,128)S(1)}, u32[]{:S(2)}, u32[]{:S(2)}) collective-permute-start(f32[2,4,17,128]{3,2,1,0:T(8,128)S(1)} %pad_maximum_fusion.7), channel_id=1, source_target_pairs={{0,8},{4,12},{8,0},{12,4},{16,24},{20,28},{24,16},{28,20},{1,9},{5... | collective-permute-start | bytes 208904 | tf_op jit(solution)/shard_map/ppermute | solution.py:14
  99.9 6.6 %collective-permute-start.34 = (f32[8,1280]{1,0:T(8,128)S(1)}, f32[8,1280]{1,0:T(8,128)S(1)}, u32[]{:S(2)}, u32[]{:S(2)}) collective-permute-start(f32[8,1280]{1,0:T(8,128)S(1)} %add.373), channel_id=1, source_target_pairs={{0,8},{4,12},{8,0},{12,4},{16,24},{20,28},{24,16},{28,20},{1,9},{5... | collective-permute-start | bytes 122888 | tf_op jit(solution)/shard_map/ppermute | solution.py:14
  101.9 80.9 %all-to-all-start = ((bf16[8,128,640]{1,2,0:T(8,128)(2,1)}), bf16[8,128,640]{1,2,0:T(8,128)(2,1)S(1)}, u32[]{:S(2)}, u32[]{:S(2)}) async-start(bf16[8,128,640]{1,2,0:T(8,128)(2,1)} %maximum_bitcast_fusion), calls=%async_computation | async-start | bytes 2621440 | tf_op jit(solution)/shard_map/all_to_all | solution.py:101
  106.4 39.8 %copy-start.20 = (pred[8]{0:T(512)(128)(4,1)S(1)}, pred[8]{0:T(512)(128)(4,1)}, u32[]{:S(2)}) copy-start(pred[8]{0:T(512)(128)(4,1)} %compare_and_fusion) | copy-start | bytes 28
  106.5 37.1 %collective-permute-start.35 = (f32[8,1280]{1,0:T(8,128)S(1)}, f32[8,1280]{1,0:T(8,128)S(1)}, u32[]{:S(2)}, u32[]{:S(2)}) collective-permute-start(f32[8,1280]{1,0:T(8,128)S(1)} %add.374), channel_id=1, source_target_pairs={{0,16},{4,20},{8,24},{12,28},{16,0},{20,4},{24,8},{28,12},{1,17},{... | collective-permute-start | bytes 122888 | tf_op jit(solution)/shard_map/ppermute | solution.py:14
  109.5 36.2 %collective-permute-start.14 = (f32[4,4,17,128]{3,2,1,0:T(8,128)S(1)}, f32[4,4,17,128]{3,2,1,0:T(8,128)S(1)}, u32[]{:S(2)}, u32[]{:S(2)}) collective-permute-start(f32[4,4,17,128]{3,2,1,0:T(8,128)S(1)} %pad_maximum_fusion.5), channel_id=1, source_target_pairs={{0,16},{4,20},{8,24},{12,28},{16,0},{20,4},{24,8},{28,12},{1,17},{... | collective-permute-start | bytes 417800 | tf_op jit(solution)/shard_map/ppermute | solution.py:14
  147.0 16.2 %collective-permute-start.19 = (bf16[512,640]{1,0:T(8,128)(2,1)}, bf16[512,640]{1,0:T(8,128)(2,1)S(1)}, u32[]{:S(2)}, u32[]{:S(2)}) collective-permute-start(bf16[512,640]{1,0:T(8,128)(2,1)} %collective-permute-done.18), channel_id=1, source_target_pairs={{8,0},{12,4},{9,1},{13,5},{10,2},{14,6},{11,3},{15,7}} | collective-permute-start | bytes 1966088 | tf_op jit(solution)/shard_map/ppermute | solution.py:37
  148.3 28.7 %collective-permute-start.25 = (bf16[512,640]{1,0:T(8,128)(2,1)}, bf16[512,640]{1,0:T(8,128)(2,1)S(1)}, u32[]{:S(2)}, u32[]{:S(2)}) collective-permute-start(bf16[512,640]{1,0:T(8,128)(2,1)} %collective-permute-done.22), channel_id=1, source_target_pairs={{16,24},{20,28},{17,25},{21,29},{18,26},{22,30},{19,27},{23,31}} | collective-permute-start | bytes 1966088 | tf_op jit(solution)/shard_map/ppermute | solution.py:36
  163.1 19.6 %collective-permute-start.21 = (bf16[512,640]{1,0:T(8,128)(2,1)S(1)}, bf16[512,640]{1,0:T(8,128)(2,1)}, u32[]{:S(2)}, u32[]{:S(2)}) collective-permute-start(bf16[512,640]{1,0:T(8,128)(2,1)S(1)} %collective-permute-done.19), channel_id=1, source_target_pairs={{0,4},{4,0},{1,5},{5,1},{2,6},{6,2},{3,7},{7,3}} | collective-permute-start | bytes 1966088 | tf_op jit(solution)/shard_map/ppermute | solution.py:26
  167.6 20.8 %collective-permute-start.23 = (bf16[512,640]{1,0:T(8,128)(2,1)}, bf16[512,640]{1,0:T(8,128)(2,1)}, u32[]{:S(2)}, u32[]{:S(2)}) collective-permute-start(bf16[512,640]{1,0:T(8,128)(2,1)} %collective-permute-done.22), channel_id=1, source_target_pairs={{16,20},{20,16},{24,28},{28,24},{17,21},{21,17},{25,29},{29,25},{1... | collective-permute-start | bytes 1966088 | tf_op jit(solution)/shard_map/ppermute | solution.py:26
  169.1 27.7 %collective-permute-start.24 = (bf16[512,640]{1,0:T(8,128)(2,1)}, bf16[512,640]{1,0:T(8,128)(2,1)}, u32[]{:S(2)}, u32[]{:S(2)}) collective-permute-start(bf16[512,640]{1,0:T(8,128)(2,1)} %collective-permute-done.18), channel_id=1, source_target_pairs={{0,4},{4,0},{8,12},{12,8},{1,5},{5,1},{9,13},{13,9},{2,6},{6,2},{1... | collective-permute-start | bytes 1966088 | tf_op jit(solution)/shard_map/ppermute | solution.py:26
  173.5 33.2 %collective-permute-start.27 = (bf16[512,640]{1,0:T(8,128)(2,1)}, bf16[512,640]{1,0:T(8,128)(2,1)S(1)}, u32[]{:S(2)}, u32[]{:S(2)}) collective-permute-start(bf16[512,640]{1,0:T(8,128)(2,1)} %collective-permute-done.17), channel_id=1, source_target_pairs={{0,4},{4,0},{8,12},{12,8},{16,20},{20,16},{1,5},{5,1},{9,13},{13,9... | collective-permute-start | bytes 1966088 | tf_op jit(solution)/shard_map/ppermute | solution.py:26
  177.0 29.6 %collective-permute-start.26 = (bf16[512,640]{1,0:T(8,128)(2,1)S(1)}, bf16[512,640]{1,0:T(8,128)(2,1)}, u32[]{:S(2)}, u32[]{:S(2)}) collective-permute-start(bf16[512,640]{1,0:T(8,128)(2,1)S(1)} %collective-permute-done.25), channel_id=1, source_target_pairs={{24,28},{28,24},{25,29},{29,25},{26,30},{30,26},{27,31},{31,27}} | collective-permute-start | bytes 1966088 | tf_op jit(solution)/shard_map/ppermute | solution.py:26
  182.7 26.0 %collective-permute-start.28 = (bf16[8,128,640]{1,2,0:T(8,128)(2,1)S(1)}, bf16[8,128,640]{1,2,0:T(8,128)(2,1)S(1)}, u32[]{:S(2)}, u32[]{:S(2)}) collective-permute-start(bf16[8,128,640]{1,2,0:T(8,128)(2,1)S(1)} %all-to-all-done), channel_id=1, source_target_pairs={{0,2},{1,3},{2,0},{3,1},{4,6},{5,7},{6,4},{7,5},{8,10},{9,11},{10,... | collective-permute-start | bytes 3932168 | tf_op jit(solution)/shard_map/ppermute | solution.py:14
  201.2 18.4 %collective-permute-start.29 = (bf16[8,128,640]{1,2,0:T(8,128)(2,1)S(1)}, bf16[8,128,640]{1,2,0:T(8,128)(2,1)S(1)}, u32[]{:S(2)}, u32[]{:S(2)}) collective-permute-start(bf16[8,128,640]{1,2,0:T(8,128)(2,1)S(1)} %all-to-all-done), channel_id=1, source_target_pairs={{0,1},{1,0},{2,3},{3,2},{4,5},{5,4},{6,7},{7,6},{8,9},{9,8},{10,11... | collective-permute-start | bytes 3932168 | tf_op jit(solution)/shard_map/ppermute | solution.py:14
  208.7 13.5 %collective-permute-start.30 = (bf16[8,128,640]{1,2,0:T(8,128)(2,1)S(1)}, bf16[8,128,640]{1,2,0:T(8,128)(2,1)S(1)}, u32[]{:S(2)}, u32[]{:S(2)}) collective-permute-start(bf16[8,128,640]{1,2,0:T(8,128)(2,1)S(1)} %collective-permute-done.28), channel_id=1, source_target_pairs={{0,1},{1,0},{2,3},{3,2},{4,5},{5,4},{6,7},{7,6},{8,9},{9,8},{10,11... | collective-permute-start | bytes 3932168 | tf_op jit(solution)/shard_map/ppermute | solution.py:14
  (12 other events, 27.6 us)

commit v2 on v1

--- a/solution.py
+++ b/solution.py
@@ -97,7 +97,13 @@
         got = swap(pick(pair, 1 - high, 0).astype(bf16), 2)
         pieces.append(pick(pair, high, 0) + got.astype(f32))
     hidden = jnp.concatenate(pieces, 1)
-    full = hidden.astype(bf16).reshape(quarter, n_dp, block).transpose(1, 0, 2)
+    full = jnp.concatenate(
+        [
+            piece.astype(bf16).reshape(quarter, cols // block, block).transpose(1, 0, 2)
+            for piece in pieces
+        ],
+        0,
+    )
     moved = lax.all_to_all(full, "dp", 0, 0, tiled=True)
     arrived = {0: moved}
     arrived[2] = swap(moved, 2)

time: 227 us -> 227 us (level)
    another operation x4 -> x0, other arithmetic: 3.23 us -> none
    convert_element_type x0 -> x4, other arithmetic: none -> 3.23 us  [per_device(): piece.astype(bf16).reshape(quarter, cols // block, block).transpose(1, 0, 2)]
where the time goes in v2:
time: 227 us; the launch traced here: 226 us
  waiting for transfers between devices  94.1 us (41%)
  starting transfers between devices  50.3 us (22%)
  matrix products  41.9 us (18%)
  other arithmetic  24.7 us (11%)
  local copies, waits for them, and re-layouts  13.7 us (6%)
    ppermute x23, waiting for transfers between devices, swap(): lax.ppermute(value, axis, [(i, i ^ bit) for i in range(lax.axis_size(axis...  61.9 us
    ppermute x7, waiting for transfers between devices, pair(): lax.ppermute(value, 'dp', [(i, i ^ 1) for i in range(n_dp) if first <= i...  18.1 us
    ppermute x23, starting transfers between devices, swap(): lax.ppermute(value, axis, [(i, i ^ bit) for i in range(lax.axis_size(axis...  17.2 us
    ppermute x7, starting transfers between devices, pair(): lax.ppermute(value, 'dp', [(i, i ^ 1) for i in range(n_dp) if first <= i...  16.9 us
    ppermute x3, waiting for transfers between devices, gather_rows(): lax.ppermute(down, 'dp', [(i, i - 2) for i in range(2, n_dp - 2 * (s - 1))])  14.1 us
    dot_general x4, matrix products, per_device(): jnp.dot(a_send, w, preferred_element_type=f32) + own * r_send.astype(f32)  12.4 us
    dot_general x4, matrix products, per_device(): lax.dot_general(arrived[away].reshape(n_dp * quarter, block), other.astyp...  11.8 us
    ppermute x3, starting transfers between devices, gather_rows(): lax.ppermute(up, 'dp', [(i, i + 2) for i in range(2 * (s - 1), n_dp - 2)])  7.61 us
  transfers between devices with their start and end apart: 37, of which 15 were waited for; matrix products, arithmetic and copies ran while one was open for 33% of the time, Pallas kernels for 0%

profile of v2, /device:TPU:0, one launch (start us, length us, event | category | flops | bytes accessed | tf_op | source)
XLA Modules:
  0.0 226.1 jit_solution(15379375459621125666)
XLA Ops:
  0.6 3.0 %collective-permute-start.15 = (bf16[512,640]{1,0:T(8,128)(2,1)}, bf16[512,640]{1,0:T(8,128)(2,1)}, u32[]{:S(2)}, u32[]{:S(2)}) collective-permute-start(bf16[512,640]{1,0:T(8,128)(2,1)} %param.9), channel_id=1, source_target_pairs={{0,4},{4,0},{8,12},{12,8},{16,20},{20,16},{24,28},{28,24},{1,5},{5... | collective-permute-start | bytes 1966088 | tf_op jit(solution)/shard_map/ppermute | solution.py:26
  5.0 5.4 %collective-permute-start.16 = (bf16[512,640]{1,0:T(8,128)(2,1)}, bf16[512,640]{1,0:T(8,128)(2,1)}, u32[]{:S(2)}, u32[]{:S(2)}) collective-permute-start(bf16[512,640]{1,0:T(8,128)(2,1)} %param.9), channel_id=1, source_target_pairs={{0,8},{4,12},{8,16},{12,20},{16,24},{20,28},{1,9},{5,13},{9,17},{1... | collective-permute-start | bytes 1966088 | tf_op jit(solution)/shard_map/ppermute | solution.py:36
  11.9 3.4 %convert_multiply_fusion.7 = (f32[2,1,128,1280]{3,2,0,1:T(8,128)S(1)}, f32[2,1,128,1280]{3,2,0,1:T(8,128)}, f32[2,1,128,1280]{3,2,0,1:T(8,128)}, f32[2,1,128,128...) fusion(f32[]{:T(128)S(6)} %convert_element_type.155, ...), kind=kLoop, calls=%fused_computation.27 | loop fusion | flops 3276800 | bytes 11796504 | tf_op jit(solution)/shard_map/mul | solution.py:93
  15.3 3.0 %fusion.4 = bf16[256,1280]{1,0:T(8,128)(2,1)} fusion(f32[256,1280]{1,0:T(8,128)S(1)} %bitcast.217, bf16[256,640]{1,0:T(8,128)(2,1)S(1)} %bitcast.206, bf16[640,5120]{1,0:T(8,128)(2,1)} %param.11), kind=kOutput, calls=%fused_computation.20 | convolution fusion | flops 420085760 | bytes 3932160 | tf_op jit(solution)/shard_map/dot_general | solution.py:93
  20.1 3.5 %fusion.5 = bf16[256,1280]{1,0:T(8,128)(2,1)} fusion(f32[256,1280]{1,0:T(8,128)} %bitcast.216, bf16[256,640]{1,0:T(8,128)(2,1)S(1)} %bitcast.207, bf16[640,5120]{1,0:T(8,128)(2,1)} %param.11), kind=kOutput, calls=%fused_computation.21 | convolution fusion | flops 420085760 | bytes 3932160 | tf_op jit(solution)/shard_map/dot_general | solution.py:93
  23.6 3.0 %fusion.6 = bf16[256,1280]{1,0:T(8,128)(2,1)} fusion(f32[256,1280]{1,0:T(8,128)S(1)} %bitcast.215, bf16[256,640]{1,0:T(8,128)(2,1)S(1)} %bitcast.208, bf16[640,5120]{1,0:T(8,128)(2,1)} %param.11), kind=kOutput, calls=%fused_computation.22 | convolution fusion | flops 420085760 | bytes 3932160 | tf_op jit(solution)/shard_map/dot_general | solution.py:93
  26.6 3.0 %fusion.7 = bf16[256,1280]{1,0:T(8,128)(2,1)} fusion(f32[256,1280]{1,0:T(8,128)S(1)} %bitcast.214, bf16[256,640]{1,0:T(8,128)(2,1)S(1)} %bitcast.209, bf16[640,5120]{1,0:T(8,128)(2,1)} %param.11), kind=kOutput, calls=%fused_computation.23 | convolution fusion | flops 420085760 | bytes 3932160 | tf_op jit(solution)/shard_map/dot_general | solution.py:93
  29.6 2.7 %broadcast_in_dim.115 = bf16[8,512,640]{2,1,0:T(8,128)(2,1)} broadcast(bf16[]{:T(256)} %constant.230.clone.1), dimensions={} | broadcast | bytes 5242882 | tf_op jit(solution)/shard_map/broadcast_in_dim | solution.py:30
  33.7 1.6 collective-permute-start.1
  35.3 4.6 %collective-permute-done.1 = f32[2,9,1280]{2,1,0:T(8,128)S(1)} collective-permute-done((f32[2,9,1280]{2,1,0:T(8,128)S(1)}, f32[2,9,1280]{2,1,0:T(8,128)S(1)}, u32[]{:S(2)}, u32[]{:S(2)}) %collective-permute-start.1) | collective-permute-done | bytes 92192 | tf_op jit(solution)/shard_map/ppermute | solution.py:14
  40.6 2.4 %convert_add_fusion.3 = f32[256,1280]{1,0:T(8,128)S(1)} fusion(bf16[256,1280]{1,0:T(8,128)(2,1)} %collective-permute-done.2, f32[256,1280]{1,0:T(8,128)S(1)} %bitcast.213, bf16[256,640]{1,0:T(8,128)(2,1)S(1)} %bitcast.202, bf16[640,5120]{1,0:T(8,128)(2,1)} %param.11), kind=kOutput, calls=%fused_computation.63 | convolution fusion | flops 420413440 | bytes 5242880 | tf_op jit(solution)/shard_map/dot_general | solution.py:95
  44.0 1.6 collective-permute-start.3
  47.7 1.6 collective-permute-start.7
  49.3 2.0 bitcast_dynamic-update-slice_fusion.6
  51.9 2.7 %collective-permute-done.3 = bf16[128,1280]{1,0:T(8,128)(2,1)S(1)} collective-permute-done((bf16[128,1280]{1,0:T(8,128)(2,1)S(1)}, bf16[128,1280]{1,0:T(8,128)(2,1)S(1)}, u32[]{:S(2)}, u32[]{:S(2)}) %collective-permute-start.3) | collective-permute-done | bytes 327712 | tf_op jit(solution)/shard_map/ppermute | solution.py:14
  58.4 3.3 %collective-permute-done.5 = bf16[128,1280]{1,0:T(8,128)(2,1)S(1)} collective-permute-done((bf16[128,1280]{1,0:T(8,128)(2,1)S(1)}, bf16[128,1280]{1,0:T(8,128)(2,1)S(1)}, u32[]{:S(2)}, u32[]{:S(2)}) %collective-permute-start.5) | collective-permute-done | bytes 327712 | tf_op jit(solution)/shard_map/ppermute | solution.py:14
  64.0 4.7 %collective-permute-done.7 = bf16[128,1280]{1,0:T(8,128)(2,1)S(1)} collective-permute-done((bf16[128,1280]{1,0:T(8,128)(2,1)S(1)}, bf16[128,1280]{1,0:T(8,128)(2,1)S(1)}, u32[]{:S(2)}, u32[]{:S(2)}) %collective-permute-start.7) | collective-permute-done | bytes 327712 | tf_op jit(solution)/shard_map/ppermute | solution.py:14
  69.5 5.7 %collective-permute-done.9 = bf16[128,1280]{1,0:T(8,128)(2,1)S(1)} collective-permute-done((bf16[128,1280]{1,0:T(8,128)(2,1)S(1)}, bf16[128,1280]{1,0:T(8,128)(2,1)S(1)}, u32[]{:S(2)}, u32[]{:S(2)}) %collective-permute-start.9) | collective-permute-done | bytes 327712 | tf_op jit(solution)/shard_map/ppermute | solution.py:14
  77.0 3.6 %broadcast_multiply_fusion = (f32[8,128]{1,0:T(8,128)S(1)}, f32[8,128]{1,0:T(8,128)S(1)}) fusion(f32[128]{0:T(128)S(1)} %add_rsqrt_fusion.1, f32[8,5120]{1,0:T(8,128)S(1)} %slice_multiply_fusion, f32[128,1280]{1,0:T(8,128)} %copy-done.8, f32[128,1280]{1,0:T(8,128)} %copy-done.7, f32[128,1280]{1,0:T(8,128)} %copy-done.6, f32[128,1280]{1,0:T(8,128)S(1)} %get-tuple-element.7), kind=kOutput, calls=%fused_computation.159 | convolution fusion | flops 64881664 | bytes 2793984 | tf_op jit(solution)/shard_map/dot_general | solution.py:114
  81.2 2.2 copy.45
  83.7 4.0 %fusion.56 = f32[8,2,2,1280]{3,0,2,1:T(8,128)S(1)} fusion(f32[2,2,1280,128]{3,2,1,0:T(8,128)} %bitcast.201, f32[8,128,1,1]{1,0,2,3:T(8,128)S(1)} %reshape.396), kind=kOutput, calls=%fused_computation.146 | convolution fusion | flops 62914560 | bytes 2789376 | tf_op jit(solution)/shard_map/dot_general | solution.py:134
  87.7 1.6 collective-permute-start.11
  91.7 1.6 collective-permute-start.32
  93.8 1.9 collective-permute-done.32
  101.9 4.6 %all-to-all-start = ((bf16[8,128,640]{1,2,0:T(8,128)(2,1)}), bf16[8,128,640]{1,2,0:T(8,128)(2,1)S(1)}, u32[]{:S(2)}, u32[]{:S(2)}) async-start(bf16[8,128,640]{1,2,0:T(8,128)(2,1)} %pad_maximum_fusion.1), calls=%async_computation | async-start | bytes 2621440 | tf_op jit(solution)/shard_map/all_to_all | solution.py:107
  106.5 3.0 %collective-permute-start.35 = (f32[8,1280]{1,0:T(8,128)S(1)}, f32[8,1280]{1,0:T(8,128)S(1)}, u32[]{:S(2)}, u32[]{:S(2)}) collective-permute-start(f32[8,1280]{1,0:T(8,128)S(1)} %add.374), channel_id=1, source_target_pairs={{0,16},{4,20},{8,24},{12,28},{16,0},{20,4},{24,8},{28,12},{1,17},{... | collective-permute-start | bytes 122888 | tf_op jit(solution)/shard_map/ppermute | solution.py:14
  109.6 34.0 %collective-permute-done.35 = f32[8,1280]{1,0:T(8,128)S(1)} collective-permute-done((f32[8,1280]{1,0:T(8,128)S(1)}, f32[8,1280]{1,0:T(8,128)S(1)}, u32[]{:S(2)}, u32[]{:S(2)}) %collective-permute-start.35) | collective-permute-done | bytes 40992 | tf_op jit(solution)/shard_map/ppermute | solution.py:14
  149.0 14.1 %collective-permute-done.19 = bf16[512,640]{1,0:T(8,128)(2,1)S(1)} collective-permute-done((bf16[512,640]{1,0:T(8,128)(2,1)}, bf16[512,640]{1,0:T(8,128)(2,1)S(1)}, u32[]{:S(2)}, u32[]{:S(2)}) %collective-permute-start.19) | collective-permute-done | bytes 655392 | tf_op jit(solution)/shard_map/ppermute | solution.py:37
  163.1 3.5 %collective-permute-start.21 = (bf16[512,640]{1,0:T(8,128)(2,1)S(1)}, bf16[512,640]{1,0:T(8,128)(2,1)}, u32[]{:S(2)}, u32[]{:S(2)}) collective-permute-start(bf16[512,640]{1,0:T(8,128)(2,1)S(1)} %collective-permute-done.19), channel_id=1, source_target_pairs={{0,4},{4,0},{1,5},{5,1},{2,6},{6,2},{3,7},{7,3}} | collective-permute-start | bytes 1966088 | tf_op jit(solution)/shard_map/ppermute | solution.py:26
  167.6 1.5 collective-permute-start.23
  169.1 2.3 %collective-permute-start.24 = (bf16[512,640]{1,0:T(8,128)(2,1)}, bf16[512,640]{1,0:T(8,128)(2,1)}, u32[]{:S(2)}, u32[]{:S(2)}) collective-permute-start(bf16[512,640]{1,0:T(8,128)(2,1)} %collective-permute-done.18), channel_id=1, source_target_pairs={{0,4},{4,0},{8,12},{12,8},{1,5},{5,1},{9,13},{13,9},{2,6},{6,2},{1... | collective-permute-start | bytes 1966088 | tf_op jit(solution)/shard_map/ppermute | solution.py:26
  171.4 2.1 bitcast_dynamic-update-slice_fusion.5
  173.5 3.5 %collective-permute-start.27 = (bf16[512,640]{1,0:T(8,128)(2,1)}, bf16[512,640]{1,0:T(8,128)(2,1)S(1)}, u32[]{:S(2)}, u32[]{:S(2)}) collective-permute-start(bf16[512,640]{1,0:T(8,128)(2,1)} %collective-permute-done.17), channel_id=1, source_target_pairs={{0,4},{4,0},{8,12},{12,8},{16,20},{20,16},{1,5},{5,1},{9,13},{13,9... | collective-permute-start | bytes 1966088 | tf_op jit(solution)/shard_map/ppermute | solution.py:26
  177.0 1.5 collective-permute-start.26
  178.6 4.2 %collective-permute-done.21 = bf16[512,640]{1,0:T(8,128)(2,1)} collective-permute-done((bf16[512,640]{1,0:T(8,128)(2,1)S(1)}, bf16[512,640]{1,0:T(8,128)(2,1)}, u32[]{:S(2)}, u32[]{:S(2)}) %collective-permute-start.21) | collective-permute-done | bytes 655392 | tf_op jit(solution)/shard_map/ppermute | solution.py:26
  183.8 2.3 %bitcast_dynamic-update-slice_fusion.4 = bf16[8,512,640]{2,1,0:T(8,128)(2,1)} fusion(bf16[8,512,640]{2,1,0:T(8,128)(2,1)} %bitcast_dynamic-update-slice_fusion.5, s32[]{:T(128)S(6)} %select_n.224, bf16[512,640]{1,0:T(8,128)(2,1)} %collective-permute-done.20, bf16[512,640]{1,0:T(8,128)(2,1)} %collective-permute-done.21), kind=kLoop, calls=%fused_computation.68 | loop fusion | flops 1310720 | bytes 1966084 | tf_op jit(solution)/shard_map/jit(dynamic_update_index_in_dim)/dynamic_update_slice | solution.py:45
  186.1 2.3 %bitcast_dynamic-update-slice_fusion.3 = bf16[8,512,640]{2,1,0:T(8,128)(2,1)} fusion(bf16[8,512,640]{2,1,0:T(8,128)(2,1)} %bitcast_dynamic-update-slice_fusion.4, s32[]{:T(128)S(6)} %select_n.226, bf16[512,640]{1,0:T(8,128)(2,1)} %collective-permute-done.22, bf16[512,640]{1,0:T(8,128)(2,1)} %collective-permute-done.18), kind=kLoop, calls=%fused_computation.67 | loop fusion | flops 1310720 | bytes 1966084 | tf_op jit(solution)/shard_map/jit(dynamic_update_index_in_dim)/dynamic_update_slice | solution.py:44
  188.4 8.4 %collective-permute-done.24 = bf16[512,640]{1,0:T(8,128)(2,1)} collective-permute-done((bf16[512,640]{1,0:T(8,128)(2,1)}, bf16[512,640]{1,0:T(8,128)(2,1)}, u32[]{:S(2)}, u32[]{:S(2)}) %collective-permute-start.24) | collective-permute-done | bytes 655392 | tf_op jit(solution)/shard_map/ppermute | solution.py:26
  196.8 2.3 %bitcast_dynamic-update-slice_fusion.2 = bf16[8,512,640]{2,1,0:T(8,128)(2,1)} fusion(bf16[8,512,640]{2,1,0:T(8,128)(2,1)} %bitcast_dynamic-update-slice_fusion.3, s32[]{:T(128)S(6)} %select_n.227, bf16[512,640]{1,0:T(8,128)(2,1)} %collective-permute-done.23, bf16[512,640]{1,0:T(8,128)(2,1)} %collective-permute-done.24), kind=kLoop, calls=%fused_computation.66 | loop fusion | flops 1310720 | bytes 1966084 | tf_op jit(solution)/shard_map/jit(dynamic_update_index_in_dim)/dynamic_update_slice | solution.py:45
  199.1 2.1 bitcast_dynamic-update-slice_fusion.1
  201.2 5.5 %collective-permute-done.27 = bf16[512,640]{1,0:T(8,128)(2,1)S(1)} collective-permute-done((bf16[512,640]{1,0:T(8,128)(2,1)}, bf16[512,640]{1,0:T(8,128)(2,1)S(1)}, u32[]{:S(2)}, u32[]{:S(2)}) %collective-permute-start.27) | collective-permute-done | bytes 655392 | tf_op jit(solution)/shard_map/ppermute | solution.py:26
  206.6 2.1 bitcast_dynamic-update-slice_fusion
  208.7 3.3 %fusion.41 = f32[16,640]{1,0:T(8,128)S(1)} fusion(bf16[4096,640]{1,0:T(8,128)(2,1)} %bitcast.52, bf16[8,4096]{1,0:T(8,128)(2,1)S(1)} %get-tuple-element.4, bf16[8,4096]{1,0:T(8,128)(2,1)S(1)} %get-tuple-element.5), kind=kOutput, calls=%fused_computation.93 | convolution fusion | flops 84148224 | bytes 5414912 | tf_op jit(solution)/shard_map/dot_general | solution.py:172
  212.0 2.2 fusion.45
  214.3 2.6 %fusion.16 = f32[640,640,1]{1,0,2:T(8,128)S(1)} fusion(bf16[8,128,640]{1,2,0:T(8,128)(2,1)S(1)} %all-to-all-done, f32[8,128]{1,0:T(8,128)S(1)} %bitcast.237, bf16[8,4,128,640]{3,2,1,0:T(8,128)(2,1)} %bitcast.61, s32[]{:T(128)S(6)} %select_n.195), kind=kOutput, calls=%fused_computation.44 | convolution fusion | flops 840826880 | bytes 4263940 | tf_op jit(solution)/shard_map/dot_general | solution.py:183
  216.9 2.6 %fusion.18 = f32[640,640,1]{1,0,2:T(8,128)S(1)} fusion(bf16[8,128,640]{1,2,0:T(8,128)(2,1)S(1)} %collective-permute-done.28, f32[8,128]{1,0:T(8,128)S(1)} %bitcast.236, bf16[8,4,128,640]{3,2,1,0:T(8,128)(2,1)} %bitcast.61, s32[]{:T(128)S(6)} %select_n.199), kind=kOutput, calls=%fused_computation.45 | convolution fusion | flops 840826880 | bytes 4263940 | tf_op jit(solution)/shard_map/dot_general | solution.py:183
  219.6 2.7 %fusion.20 = f32[640,640,1]{1,0,2:T(8,128)S(1)} fusion(bf16[8,128,640]{1,2,0:T(8,128)(2,1)S(1)} %collective-permute-done.29, f32[8,128]{1,0:T(8,128)S(1)} %bitcast.235, bf16[8,4,128,640]{3,2,1,0:T(8,128)(2,1)} %bitcast.61, s32[]{:T(128)S(6)} %select_n.197), kind=kOutput, calls=%fused_computation.46 | convolution fusion | flops 840826880 | bytes 4263940 | tf_op jit(solution)/shard_map/dot_general | solution.py:183
  222.2 3.8 %bitcast_subtract_fusion = f32[640,640]{1,0:T(8,128)} fusion(f32[640,640,1]{1,0,2:T(8,128)S(1)} %fusion.20, f32[640,640,1]{1,0,2:T(8,128)S(1)} %fusion.18, f32[640,640]{1,0:T(8,128)S(1)} %fusion.45, f32[640,640,1]{1,0,2:T(8,128)S(1)} %fusion.16, bf16[8,128,640]{1,2,0:T(8,128)(2,1)S(1)} %collective-permute-done.30, f32[8,128]{1,0:T(8,128)S(1)} %bitcast.234, ...), kind=kOutput, calls=%fused_computation.32 | convolution fusion | flops 842465280 | bytes 10817540 | tf_op jit(solution)/shard_map/dot_general | solution.py:183
  (188 shorter events, 36.1 us)
Async XLA Ops:
  0.6 47.1 %collective-permute-start.15 = (bf16[512,640]{1,0:T(8,128)(2,1)}, bf16[512,640]{1,0:T(8,128)(2,1)}, u32[]{:S(2)}, u32[]{:S(2)}) collective-permute-start(bf16[512,640]{1,0:T(8,128)(2,1)} %param.9), channel_id=1, source_target_pairs={{0,4},{4,0},{8,12},{12,8},{16,20},{20,16},{24,28},{28,24},{1,5},{5... | collective-permute-start | bytes 1966088 | tf_op jit(solution)/shard_map/ppermute | solution.py:26
  3.7 53.3 %collective-permute-start.17 = (bf16[512,640]{1,0:T(8,128)(2,1)}, bf16[512,640]{1,0:T(8,128)(2,1)}, u32[]{:S(2)}, u32[]{:S(2)}) collective-permute-start(bf16[512,640]{1,0:T(8,128)(2,1)} %param.9), channel_id=1, source_target_pairs={{8,0},{12,4},{16,8},{20,12},{24,16},{28,20},{9,1},{13,5},{17,9},{2... | collective-permute-start | bytes 1966088 | tf_op jit(solution)/shard_map/ppermute | solution.py:37
  5.0 46.4 %collective-permute-start.16 = (bf16[512,640]{1,0:T(8,128)(2,1)}, bf16[512,640]{1,0:T(8,128)(2,1)}, u32[]{:S(2)}, u32[]{:S(2)}) collective-permute-start(bf16[512,640]{1,0:T(8,128)(2,1)} %param.9), channel_id=1, source_target_pairs={{0,8},{4,12},{8,16},{12,20},{16,24},{20,28},{1,9},{5,13},{9,17},{1... | collective-permute-start | bytes 1966088 | tf_op jit(solution)/shard_map/ppermute | solution.py:36
  18.3 21.8 %collective-permute-start.2 = (bf16[256,1280]{1,0:T(8,128)(2,1)}, bf16[256,1280]{1,0:T(8,128)(2,1)}, u32[]{:S(2)}, u32[]{:S(2)}) collective-permute-start(bf16[256,1280]{1,0:T(8,128)(2,1)} %fusion.4), channel_id=1, source_target_pairs={{0,1},{1,0},{2,3},{3,2},{4,5},{5,4},{6,7},{7,6},{8,9},{9,8},{10,11... | collective-permute-start | bytes 1966088 | tf_op jit(solution)/shard_map/ppermute | solution.py:14
  18.3 15.3 %collective-permute-start = (f32[1,9,1280]{2,1,0:T(8,128)S(1)}, f32[1,9,1280]{2,1,0:T(8,128)S(1)}, u32[]{:S(2)}, u32[]{:S(2)}) collective-permute-start(f32[1,9,1280]{2,1,0:T(8,128)S(1)} %maximum_bitcast_fusion), channel_id=1, source_target_pairs={{0,1},{1,0},{2,3},{3,2},{4,5},{5,4},{6,7},{7,6},{8,9},{9,8},{10,11... | collective-permute-start | bytes 138248 | tf_op jit(solution)/shard_map/ppermute | solution.py:14
  20.1 3.5 %copy-start.4 = (f32[2,1,128,1280]{3,2,0,1:T(8,128)S(1)}, f32[2,1,128,1280]{3,2,0,1:T(8,128)}, u32[]{:S(2)}) copy-start(f32[2,1,128,1280]{3,2,0,1:T(8,128)} %get-tuple-element.25) | copy-start | bytes 3932164
  29.6 13.6 %slice-start = ((s8[6553600]{0:T(1024)(128)(4,1)}), s8[2359296]{0:T(1024)(128)(4,1)S(1)}, s32[]{:S(2)}) async-start(s8[6553600]{0:T(1024)(128)(4,1)} %bitcast.199), calls=%async_computation.1 | async-start | bytes 4718592
  33.6 6.4 %copy-start.15 = (bf16[256,1280]{1,0:T(8,128)(2,1)S(1)}, bf16[256,1280]{1,0:T(8,128)(2,1)}, u32[]{:S(2)}) copy-start(bf16[256,1280]{1,0:T(8,128)(2,1)} %fusion.6) | copy-start | bytes 1966084
  33.7 6.2 %collective-permute-start.1 = (f32[2,9,1280]{2,1,0:T(8,128)S(1)}, f32[2,9,1280]{2,1,0:T(8,128)S(1)}, u32[]{:S(2)}, u32[]{:S(2)}) collective-permute-start(f32[2,9,1280]{2,1,0:T(8,128)S(1)} %pad_maximum_fusion.7), channel_id=1, source_target_pairs={{0,2},{1,3},{2,0},{3,1},{4,6},{5,7},{6,4},{7,5},{8,10},{9,11},{10,... | collective-permute-start | bytes 276488 | tf_op jit(solution)/shard_map/ppermute | solution.py:14
  35.2 5.4 %copy-start.3 = (f32[2,1,128,1280]{3,2,0,1:T(8,128)S(1)}, f32[2,1,128,1280]{3,2,0,1:T(8,128)}, u32[]{:S(2)}) copy-start(f32[2,1,128,1280]{3,2,0,1:T(8,128)} %get-tuple-element.27) | copy-start | bytes 3932164
  35.3 8.0 %slice-start.1 = ((s8[6553600]{0:T(1024)(128)(4,1)}), s8[4194304]{0:T(1024)(128)(4,1)S(1)}, s32[]{:S(2)}) async-start(s8[6553600]{0:T(1024)(128)(4,1)} %bitcast.199), calls=%async_computation.2 | async-start | bytes 8388608
  39.9 3.2 %collective-permute-start.4 = (bf16[256,1280]{1,0:T(8,128)(2,1)}, bf16[256,1280]{1,0:T(8,128)(2,1)S(1)}, u32[]{:S(2)}, u32[]{:S(2)}) collective-permute-start(bf16[256,1280]{1,0:T(8,128)(2,1)} %fusion.5), channel_id=1, source_target_pairs={{0,1},{1,0},{2,3},{3,2},{4,5},{5,4},{6,7},{7,6},{8,9},{9,8},{10,11... | collective-permute-start | bytes 1966088 | tf_op jit(solution)/shard_map/ppermute | solution.py:14
  40.0 37.0 %copy-start.16 = (f32[8,5120]{1,0:T(8,128)}, f32[8,5120]{1,0:T(8,128)S(1)}, u32[]{:S(2)}) copy-start(f32[8,5120]{1,0:T(8,128)S(1)} %slice_multiply_fusion) | copy-start | bytes 491524
  40.1 3.9 %collective-permute-start.6 = (bf16[256,1280]{1,0:T(8,128)(2,1)S(1)}, bf16[256,1280]{1,0:T(8,128)(2,1)S(1)}, u32[]{:S(2)}, u32[]{:S(2)}) collective-permute-start(bf16[256,1280]{1,0:T(8,128)(2,1)S(1)} %copy-done.15), channel_id=1, source_target_pairs={{0,1},{1,0},{2,3},{3,2},{4,5},{5,4},{6,7},{7,6},{8,9},{9,8},{10,11... | collective-permute-start | bytes 1966088 | tf_op jit(solution)/shard_map/ppermute | solution.py:14
  43.1 3.3 %collective-permute-start.8 = (bf16[256,1280]{1,0:T(8,128)(2,1)S(1)}, bf16[256,1280]{1,0:T(8,128)(2,1)S(1)}, u32[]{:S(2)}, u32[]{:S(2)}) collective-permute-start(bf16[256,1280]{1,0:T(8,128)(2,1)S(1)} %copy-done.14), channel_id=1, source_target_pairs={{0,1},{1,0},{2,3},{3,2},{4,5},{5,4},{6,7},{7,6},{8,9},{9,8},{10,11... | collective-permute-start | bytes 1966088 | tf_op jit(solution)/shard_map/ppermute | solution.py:14
  44.0 10.6 %collective-permute-start.3 = (bf16[128,1280]{1,0:T(8,128)(2,1)S(1)}, bf16[128,1280]{1,0:T(8,128)(2,1)S(1)}, u32[]{:S(2)}, u32[]{:S(2)}) collective-permute-start(bf16[128,1280]{1,0:T(8,128)(2,1)S(1)} %fusion.37), channel_id=1, source_target_pairs={{0,2},{1,3},{2,0},{3,1},{4,6},{5,7},{6,4},{7,5},{8,10},{9,11},{10,... | collective-permute-start | bytes 983048 | tf_op jit(solution)/shard_map/ppermute | solution.py:14
  46.4 15.3 %collective-permute-start.5 = (bf16[128,1280]{1,0:T(8,128)(2,1)S(1)}, bf16[128,1280]{1,0:T(8,128)(2,1)S(1)}, u32[]{:S(2)}, u32[]{:S(2)}) collective-permute-start(bf16[128,1280]{1,0:T(8,128)(2,1)S(1)} %fusion.38), channel_id=1, source_target_pairs={{0,2},{1,3},{2,0},{3,1},{4,6},{5,7},{6,4},{7,5},{8,10},{9,11},{10,... | collective-permute-start | bytes 983048 | tf_op jit(solution)/shard_map/ppermute | solution.py:14
  47.7 21.0 %collective-permute-start.7 = (bf16[128,1280]{1,0:T(8,128)(2,1)S(1)}, bf16[128,1280]{1,0:T(8,128)(2,1)S(1)}, u32[]{:S(2)}, u32[]{:S(2)}) collective-permute-start(bf16[128,1280]{1,0:T(8,128)(2,1)S(1)} %fusion.39), channel_id=1, source_target_pairs={{0,2},{1,3},{2,0},{3,1},{4,6},{5,7},{6,4},{7,5},{8,10},{9,11},{10,... | collective-permute-start | bytes 983048 | tf_op jit(solution)/shard_map/ppermute | solution.py:14
  51.4 23.9 %collective-permute-start.9 = (bf16[128,1280]{1,0:T(8,128)(2,1)S(1)}, bf16[128,1280]{1,0:T(8,128)(2,1)S(1)}, u32[]{:S(2)}, u32[]{:S(2)}) collective-permute-start(bf16[128,1280]{1,0:T(8,128)(2,1)S(1)} %fusion.40), channel_id=1, source_target_pairs={{0,2},{1,3},{2,0},{3,1},{4,6},{5,7},{6,4},{7,5},{8,10},{9,11},{10,... | collective-permute-start | bytes 983048 | tf_op jit(solution)/shard_map/ppermute | solution.py:14
  54.7 118.8 %collective-permute-start.20 = (bf16[512,640]{1,0:T(8,128)(2,1)}, bf16[512,640]{1,0:T(8,128)(2,1)}, u32[]{:S(2)}, u32[]{:S(2)}) collective-permute-start(bf16[512,640]{1,0:T(8,128)(2,1)} %collective-permute-done.16), channel_id=1, source_target_pairs={{8,12},{12,8},{16,20},{20,16},{24,28},{28,24},{9,13},{13,9},{17,21... | collective-permute-start | bytes 1966088 | tf_op jit(solution)/shard_map/ppermute | solution.py:26
  56.9 91.3 %collective-permute-start.22 = (bf16[512,640]{1,0:T(8,128)(2,1)}, bf16[512,640]{1,0:T(8,128)(2,1)}, u32[]{:S(2)}, u32[]{:S(2)}) collective-permute-start(bf16[512,640]{1,0:T(8,128)(2,1)} %collective-permute-done.16), channel_id=1, source_target_pairs={{8,16},{12,20},{16,24},{20,28},{9,17},{13,21},{17,25},{21,29},{10,... | collective-permute-start | bytes 1966088 | tf_op jit(solution)/shard_map/ppermute | solution.py:36
  61.7 85.3 %collective-permute-start.18 = (bf16[512,640]{1,0:T(8,128)(2,1)}, bf16[512,640]{1,0:T(8,128)(2,1)}, u32[]{:S(2)}, u32[]{:S(2)}) collective-permute-start(bf16[512,640]{1,0:T(8,128)(2,1)} %collective-permute-done.17), channel_id=1, source_target_pairs={{8,0},{12,4},{16,8},{20,12},{9,1},{13,5},{17,9},{21,13},{10,2},{14... | collective-permute-start | bytes 1966088 | tf_op jit(solution)/shard_map/ppermute | solution.py:37
  64.0 12.6 %copy-start.6 = (f32[128,1280]{1,0:T(8,128)}, f32[128,1280]{1,0:T(8,128)S(1)}, u32[]{:S(2)}) copy-start(f32[128,1280]{1,0:T(8,128)S(1)} %get-tuple-element.9) | copy-start | bytes 1966084
  69.5 7.0 %copy-start.7 = (f32[128,1280]{1,0:T(8,128)}, f32[128,1280]{1,0:T(8,128)S(1)}, u32[]{:S(2)}) copy-start(f32[128,1280]{1,0:T(8,128)S(1)} %get-tuple-element.11) | copy-start | bytes 1966084
  83.6 4.1 %collective-permute-start.10 = (f32[1,17,128]{2,1,0:T(8,128)S(1)}, f32[1,17,128]{2,1,0:T(8,128)S(1)}, u32[]{:S(2)}, u32[]{:S(2)}) collective-permute-start(f32[1,17,128]{2,1,0:T(8,128)S(1)} %fusion.49), channel_id=1, source_target_pairs={{0,1},{1,0},{2,3},{3,2},{4,5},{5,4},{6,7},{7,6},{8,9},{9,8},{10,11... | collective-permute-start | bytes 26120 | tf_op jit(solution)/shard_map/ppermute | solution.py:14
  83.7 5.9 %copy-start.10 = (bf16[128,1280]{1,0:T(8,128)(2,1)S(1)}, bf16[128,1280]{1,0:T(8,128)(2,1)}, u32[]{:S(2)}) copy-start(bf16[128,1280]{1,0:T(8,128)(2,1)} %get-tuple-element.6) | copy-start | bytes 983044
  83.7 6.1 %copy-start.11 = (bf16[128,1280]{1,0:T(8,128)(2,1)S(1)}, bf16[128,1280]{1,0:T(8,128)(2,1)}, u32[]{:S(2)}) copy-start(bf16[128,1280]{1,0:T(8,128)(2,1)} %get-tuple-element.8) | copy-start | bytes 983044
  87.7 3.9 %collective-permute-start.11 = (f32[2,17,128]{2,1,0:T(8,128)S(1)}, f32[2,17,128]{2,1,0:T(8,128)S(1)}, u32[]{:S(2)}, u32[]{:S(2)}) collective-permute-start(f32[2,17,128]{2,1,0:T(8,128)S(1)} %pad_maximum_fusion.10), channel_id=1, source_target_pairs={{0,2},{1,3},{2,0},{3,1},{4,6},{5,7},{6,4},{7,5},{8,10},{9,11},{10,... | collective-permute-start | bytes 52232 | tf_op jit(solution)/shard_map/ppermute | solution.py:14
  89.3 2.3 %collective-permute-start.31 = (f32[8,2,1280]{2,0,1:T(8,128)S(1)}, f32[8,2,1280]{2,0,1:T(8,128)S(1)}, u32[]{:S(2)}, u32[]{:S(2)}) collective-permute-start(f32[8,2,1280]{2,0,1:T(8,128)S(1)} %dynamic-slice_bitcast_fusion), channel_id=1, source_target_pairs={{0,1},{1,0},{2,3},{3,2},{4,5},{5,4},{6,7},{7,6},{8,9},{9,8},{10,11... | collective-permute-start | bytes 245768 | tf_op jit(solution)/shard_map/ppermute | solution.py:14
  91.7 4.1 %collective-permute-start.32 = (f32[8,1280]{1,0:T(8,128)S(1)}, f32[8,1280]{1,0:T(8,128)S(1)}, u32[]{:S(2)}, u32[]{:S(2)}) collective-permute-start(f32[8,1280]{1,0:T(8,128)S(1)} %dynamic-slice_bitcast_fusion.5), channel_id=1, source_target_pairs={{0,2},{1,3},{2,0},{3,1},{4,6},{5,7},{6,4},{7,5},{8,10},{9,11},{10,... | collective-permute-start | bytes 122888 | tf_op jit(solution)/shard_map/ppermute | solution.py:14
  93.3 4.3 %collective-permute-start.12 = (f32[1,4,17,128]{3,2,1,0:T(8,128)S(1)}, f32[1,4,17,128]{3,2,1,0:T(8,128)S(1)}, u32[]{:S(2)}, u32[]{:S(2)}) collective-permute-start(f32[1,4,17,128]{3,2,1,0:T(8,128)S(1)} %maximum_bitcast_fusion.1), channel_id=1, source_target_pairs={{0,4},{4,0},{8,12},{12,8},{16,20},{20,16},{24,28},{28,24},{1,5},{5... | collective-permute-start | bytes 104456 | tf_op jit(solution)/shard_map/ppermute | solution.py:14
  95.8 4.1 %collective-permute-start.33 = (f32[8,1280]{1,0:T(8,128)S(1)}, f32[8,1280]{1,0:T(8,128)S(1)}, u32[]{:S(2)}, u32[]{:S(2)}) collective-permute-start(f32[8,1280]{1,0:T(8,128)S(1)} %bitcast_add_fusion.5), channel_id=1, source_target_pairs={{0,4},{4,0},{8,12},{12,8},{16,20},{20,16},{24,28},{28,24},{1,5},{5... | collective-permute-start | bytes 122888 | tf_op jit(solution)/shard_map/ppermute | solution.py:14
  97.6 11.8 %collective-permute-start.13 = (f32[2,4,17,128]{3,2,1,0:T(8,128)S(1)}, f32[2,4,17,128]{3,2,1,0:T(8,128)S(1)}, u32[]{:S(2)}, u32[]{:S(2)}) collective-permute-start(f32[2,4,17,128]{3,2,1,0:T(8,128)S(1)} %pad_maximum_fusion.8), channel_id=1, source_target_pairs={{0,8},{4,12},{8,0},{12,4},{16,24},{20,28},{24,16},{28,20},{1,9},{5... | collective-permute-start | bytes 208904 | tf_op jit(solution)/shard_map/ppermute | solution.py:14
  99.9 6.6 %collective-permute-start.34 = (f32[8,1280]{1,0:T(8,128)S(1)}, f32[8,1280]{1,0:T(8,128)S(1)}, u32[]{:S(2)}, u32[]{:S(2)}) collective-permute-start(f32[8,1280]{1,0:T(8,128)S(1)} %add.373), channel_id=1, source_target_pairs={{0,8},{4,12},{8,0},{12,4},{16,24},{20,28},{24,16},{28,20},{1,9},{5... | collective-permute-start | bytes 122888 | tf_op jit(solution)/shard_map/ppermute | solution.py:14
  101.9 80.9 %all-to-all-start = ((bf16[8,128,640]{1,2,0:T(8,128)(2,1)}), bf16[8,128,640]{1,2,0:T(8,128)(2,1)S(1)}, u32[]{:S(2)}, u32[]{:S(2)}) async-start(bf16[8,128,640]{1,2,0:T(8,128)(2,1)} %pad_maximum_fusion.1), calls=%async_computation | async-start | bytes 2621440 | tf_op jit(solution)/shard_map/all_to_all | solution.py:107
  106.4 39.8 %copy-start.20 = (pred[8]{0:T(512)(128)(4,1)S(1)}, pred[8]{0:T(512)(128)(4,1)}, u32[]{:S(2)}) copy-start(pred[8]{0:T(512)(128)(4,1)} %compare_and_fusion) | copy-start | bytes 28
  106.5 37.1 %collective-permute-start.35 = (f32[8,1280]{1,0:T(8,128)S(1)}, f32[8,1280]{1,0:T(8,128)S(1)}, u32[]{:S(2)}, u32[]{:S(2)}) collective-permute-start(f32[8,1280]{1,0:T(8,128)S(1)} %add.374), channel_id=1, source_target_pairs={{0,16},{4,20},{8,24},{12,28},{16,0},{20,4},{24,8},{28,12},{1,17},{... | collective-permute-start | bytes 122888 | tf_op jit(solution)/shard_map/ppermute | solution.py:14
  109.5 36.2 %collective-permute-start.14 = (f32[4,4,17,128]{3,2,1,0:T(8,128)S(1)}, f32[4,4,17,128]{3,2,1,0:T(8,128)S(1)}, u32[]{:S(2)}, u32[]{:S(2)}) collective-permute-start(f32[4,4,17,128]{3,2,1,0:T(8,128)S(1)} %pad_maximum_fusion.6), channel_id=1, source_target_pairs={{0,16},{4,20},{8,24},{12,28},{16,0},{20,4},{24,8},{28,12},{1,17},{... | collective-permute-start | bytes 417800 | tf_op jit(solution)/shard_map/ppermute | solution.py:14
  147.0 16.2 %collective-permute-start.19 = (bf16[512,640]{1,0:T(8,128)(2,1)}, bf16[512,640]{1,0:T(8,128)(2,1)S(1)}, u32[]{:S(2)}, u32[]{:S(2)}) collective-permute-start(bf16[512,640]{1,0:T(8,128)(2,1)} %collective-permute-done.18), channel_id=1, source_target_pairs={{8,0},{12,4},{9,1},{13,5},{10,2},{14,6},{11,3},{15,7}} | collective-permute-start | bytes 1966088 | tf_op jit(solution)/shard_map/ppermute | solution.py:37
  148.3 28.7 %collective-permute-start.25 = (bf16[512,640]{1,0:T(8,128)(2,1)}, bf16[512,640]{1,0:T(8,128)(2,1)S(1)}, u32[]{:S(2)}, u32[]{:S(2)}) collective-permute-start(bf16[512,640]{1,0:T(8,128)(2,1)} %collective-permute-done.22), channel_id=1, source_target_pairs={{16,24},{20,28},{17,25},{21,29},{18,26},{22,30},{19,27},{23,31}} | collective-permute-start | bytes 1966088 | tf_op jit(solution)/shard_map/ppermute | solution.py:36
  163.1 19.6 %collective-permute-start.21 = (bf16[512,640]{1,0:T(8,128)(2,1)S(1)}, bf16[512,640]{1,0:T(8,128)(2,1)}, u32[]{:S(2)}, u32[]{:S(2)}) collective-permute-start(bf16[512,640]{1,0:T(8,128)(2,1)S(1)} %collective-permute-done.19), channel_id=1, source_target_pairs={{0,4},{4,0},{1,5},{5,1},{2,6},{6,2},{3,7},{7,3}} | collective-permute-start | bytes 1966088 | tf_op jit(solution)/shard_map/ppermute | solution.py:26
  167.6 20.8 %collective-permute-start.23 = (bf16[512,640]{1,0:T(8,128)(2,1)}, bf16[512,640]{1,0:T(8,128)(2,1)}, u32[]{:S(2)}, u32[]{:S(2)}) collective-permute-start(bf16[512,640]{1,0:T(8,128)(2,1)} %collective-permute-done.22), channel_id=1, source_target_pairs={{16,20},{20,16},{24,28},{28,24},{17,21},{21,17},{25,29},{29,25},{1... | collective-permute-start | bytes 1966088 | tf_op jit(solution)/shard_map/ppermute | solution.py:26
  169.1 27.7 %collective-permute-start.24 = (bf16[512,640]{1,0:T(8,128)(2,1)}, bf16[512,640]{1,0:T(8,128)(2,1)}, u32[]{:S(2)}, u32[]{:S(2)}) collective-permute-start(bf16[512,640]{1,0:T(8,128)(2,1)} %collective-permute-done.18), channel_id=1, source_target_pairs={{0,4},{4,0},{8,12},{12,8},{1,5},{5,1},{9,13},{13,9},{2,6},{6,2},{1... | collective-permute-start | bytes 1966088 | tf_op jit(solution)/shard_map/ppermute | solution.py:26
  173.5 33.2 %collective-permute-start.27 = (bf16[512,640]{1,0:T(8,128)(2,1)}, bf16[512,640]{1,0:T(8,128)(2,1)S(1)}, u32[]{:S(2)}, u32[]{:S(2)}) collective-permute-start(bf16[512,640]{1,0:T(8,128)(2,1)} %collective-permute-done.17), channel_id=1, source_target_pairs={{0,4},{4,0},{8,12},{12,8},{16,20},{20,16},{1,5},{5,1},{9,13},{13,9... | collective-permute-start | bytes 1966088 | tf_op jit(solution)/shard_map/ppermute | solution.py:26
  177.0 29.6 %collective-permute-start.26 = (bf16[512,640]{1,0:T(8,128)(2,1)S(1)}, bf16[512,640]{1,0:T(8,128)(2,1)}, u32[]{:S(2)}, u32[]{:S(2)}) collective-permute-start(bf16[512,640]{1,0:T(8,128)(2,1)S(1)} %collective-permute-done.25), channel_id=1, source_target_pairs={{24,28},{28,24},{25,29},{29,25},{26,30},{30,26},{27,31},{31,27}} | collective-permute-start | bytes 1966088 | tf_op jit(solution)/shard_map/ppermute | solution.py:26
  182.7 26.0 %collective-permute-start.28 = (bf16[8,128,640]{1,2,0:T(8,128)(2,1)S(1)}, bf16[8,128,640]{1,2,0:T(8,128)(2,1)S(1)}, u32[]{:S(2)}, u32[]{:S(2)}) collective-permute-start(bf16[8,128,640]{1,2,0:T(8,128)(2,1)S(1)} %all-to-all-done), channel_id=1, source_target_pairs={{0,2},{1,3},{2,0},{3,1},{4,6},{5,7},{6,4},{7,5},{8,10},{9,11},{10,... | collective-permute-start | bytes 3932168 | tf_op jit(solution)/shard_map/ppermute | solution.py:14
  201.2 18.4 %collective-permute-start.29 = (bf16[8,128,640]{1,2,0:T(8,128)(2,1)S(1)}, bf16[8,128,640]{1,2,0:T(8,128)(2,1)S(1)}, u32[]{:S(2)}, u32[]{:S(2)}) collective-permute-start(bf16[8,128,640]{1,2,0:T(8,128)(2,1)S(1)} %all-to-all-done), channel_id=1, source_target_pairs={{0,1},{1,0},{2,3},{3,2},{4,5},{5,4},{6,7},{7,6},{8,9},{9,8},{10,11... | collective-permute-start | bytes 3932168 | tf_op jit(solution)/shard_map/ppermute | solution.py:14
  208.7 13.5 %collective-permute-start.30 = (bf16[8,128,640]{1,2,0:T(8,128)(2,1)S(1)}, bf16[8,128,640]{1,2,0:T(8,128)(2,1)S(1)}, u32[]{:S(2)}, u32[]{:S(2)}) collective-permute-start(bf16[8,128,640]{1,2,0:T(8,128)(2,1)S(1)} %collective-permute-done.28), channel_id=1, source_target_pairs={{0,1},{1,0},{2,3},{3,2},{4,5},{5,4},{6,7},{7,6},{8,9},{9,8},{10,11... | collective-permute-start | bytes 3932168 | tf_op jit(solution)/shard_map/ppermute | solution.py:14
  (12 other events, 27.6 us)
